TPU v7x, 32 devices: a whole 2x2x4 slice. The times are simulated.
32 devices in a mesh: seq: 8 (over y, x, core), tp: 4 (over z).
Axes of the slice: x: 2, y: 2, z: 4, core: 2. Of those that a mesh axis runs over, the one named last changes fastest.
Arguments:
- hidden: bfloat16 [4096, 4096], P('seq', 'tp'), may hold values from -6 to 6
- norm_gain: float32 [4096], P('tp'), may hold values from 0.5 to 1.5
- rank_down: bfloat16 [4096, 1024], P('tp'), may hold values from -0.09375 to 0.09375
- gate_up: bfloat16 [1024, 4096], P(None, 'tp'), may hold values from -0.1875 to 0.1875
- value_up: bfloat16 [1024, 4096], P(None, 'tp'), may hold values from -0.1875 to 0.1875
- state_up: bfloat16 [1024, 1024], P(None, 'tp'), may hold values from -0.1875 to 0.1875
- step_up: bfloat16 [1024, 64], P(None, 'tp'), may hold values from -0.1875 to 0.1875
- conv_value: float32 [4, 4096], P(None, 'tp'), may hold values from -3 to 3
- conv_state: float32 [4, 1024], P(None, 'tp'), may hold values from -3 to 3
- step_bias: float32 [64], P('tp'), may hold values from -6.9 to -2.3
- decay_log: float32 [64], P('tp'), may hold values from -11 to 2.77
- skip_gain: float32 [64], P('tp'), may hold values from 0.5 to 1.5
- gate_gain: float32 [4096], P('tp'), may hold values from 0.5 to 1.5
- out_down: bfloat16 [4096, 1024], P('tp'), may hold values from -0.09375 to 0.09375
- out_up: bfloat16 [1024, 4096], P(None, 'tp'), may hold values from -0.1875 to 0.1875
Outputs:
- block_out: bfloat16 [4096, 4096], P('seq', 'tp')
All inputs are finite; a program needn't handle non-finite values.
Results may differ from a plain program's by a relative error of at most 0.012.
Values may be sent and summed in bfloat16 or wider, within the bound.
A program may use at most 64 MiB of HBM per device.

v0:
```python
import jax
import jax.numpy as jnp
from jax import lax
from jax.sharding import PartitionSpec as P

HEAD_DIM = 64
NSTATE = 128
GROUPS = 4


epsilon = 1e-05
highest = lax.Precision.HIGHEST


def shifted(shard, axis, by):
    peers = lax.axis_size(axis)
    pairs = [(i, i + by) for i in range(peers) if 0 <= i + by < peers]
    return lax.ppermute(shard, axis, pairs)


def entering(part, axis, combine, identity):
    place = lax.axis_index(axis)
    gathered = jax.tree.map(lambda a: lax.all_gather(a, axis), part)
    state = jax.tree.map(lambda a, e: jnp.zeros_like(a) + jnp.asarray(e, a.dtype), part, identity)

    def one(lap, state):
        return combine(
            state, jax.tree.map(lambda a: lax.dynamic_index_in_dim(a, lap, 0, False), gathered)
        )

    return lax.fori_loop(0, place, one, state)


def contract_rows(left, right):
    return lax.dot_general(
        left, right, (((0,), (0,)), ((), ())), preferred_element_type=jnp.float32
    )


def contract_columns(columns, rows):
    return lax.dot_general(
        columns, rows, (((0,), (1,)), ((), ())), preferred_element_type=jnp.float32
    )


def depthwise(rim_rows, current, weights):
    joined = jnp.concatenate([rim_rows, current], axis=0).astype(jnp.float32)
    length = current.shape[0]
    result = jnp.zeros(current.shape, jnp.float32)
    for offset in range(weights.shape[0]):
        result = result + weights[offset] * joined[offset : offset + length]
    return jax.nn.silu(result).astype(jnp.bfloat16)


def on_device(
    hidden,
    norm_gain,
    rank_down,
    gate_up,
    value_up,
    state_up,
    step_up,
    conv_value,
    conv_state,
    step_bias,
    decay_log,
    skip_gain,
    gate_gain,
    out_down,
    out_up,
):
    tokens = hidden.shape[0]
    tp_count = lax.axis_size("tp")
    tp_index = lax.axis_index("tp")
    model_width = hidden.shape[1] * tp_count
    hidden_wide = hidden.astype(jnp.float32)
    local_squares = jnp.sum(hidden_wide * hidden_wide, axis=1)
    scaled = (hidden_wide * norm_gain).astype(jnp.bfloat16)
    up_weights = (gate_up, value_up, state_up, step_up)
    partial_value = jnp.dot(scaled, rank_down, preferred_element_type=jnp.float32)
    summed, total_squares = lax.psum((partial_value, local_squares), "tp")
    factor = lax.rsqrt(total_squares / model_width + epsilon)
    reduced = (summed * factor[:, None]).astype(jnp.bfloat16)
    projected = tuple(
        (jnp.dot(reduced, weight, preferred_element_type=jnp.float32) for weight in up_weights)
    )
    gate_pre = projected[0].astype(jnp.bfloat16)
    value_pre = projected[1].astype(jnp.bfloat16)
    state_pre = projected[2].astype(jnp.bfloat16)
    step_pre = projected[3].astype(jnp.bfloat16)
    rim_start = tokens - conv_value.shape[0] + 1
    rim_value, rim_state = shifted((value_pre[rim_start:], state_pre[rim_start:]), "seq", 1)
    value_act = depthwise(rim_value, value_pre, conv_value)
    state_act = depthwise(rim_state, state_pre, conv_state)
    state_all = lax.all_gather(state_act, "tp", axis=1, tiled=True)
    heads_local = decay_log.shape[0]
    heads_total = heads_local * tp_count
    group_index = tp_index * heads_local // (heads_total // GROUPS)
    inward = lax.dynamic_slice_in_dim(state_all, group_index * NSTATE, NSTATE, 1).astype(
        jnp.float32
    )
    outward = lax.dynamic_slice_in_dim(
        state_all, (GROUPS + group_index) * NSTATE, NSTATE, 1
    ).astype(jnp.float32)
    step_size = jax.nn.softplus(step_pre.astype(jnp.float32) + step_bias)
    log_decay = jnp.cumsum(-jnp.exp(decay_log) * step_size, axis=0)
    values = value_act.astype(jnp.float32).reshape(tokens, heads_local, HEAD_DIM)
    coupling = jnp.dot(outward, inward.T, precision=highest)
    positions = jnp.arange(tokens)
    causal = positions[:, None] >= positions[None, :]
    spread = log_decay.T[:, :, None] - log_decay.T[:, None, :]
    attenuation = jnp.where(causal[None], jnp.exp(jnp.where(causal[None], spread, 0.0)), 0.0)
    mixing = coupling[None] * attenuation * step_size.T[:, None, :]
    within = jnp.einsum("hts,shp->thp", mixing, values, precision=highest)
    ending = jnp.exp(log_decay[-1][None, :] - log_decay) * step_size
    local_state = jnp.einsum("sh,shp,sn->hpn", ending, values, inward, precision=highest)
    local_decay = jnp.exp(log_decay[-1])

    def combine(earlier, later):
        return (earlier[0] * later[0], later[0][:, None, None] * earlier[1] + later[1])

    prefix = entering(
        (local_decay, local_state),
        "seq",
        combine,
        (jnp.ones_like(local_decay), jnp.zeros_like(local_state)),
    )
    incoming = prefix[1]
    carried_in = jnp.exp(log_decay)[:, :, None] * jnp.einsum(
        "tn,hpn->thp", outward, incoming, precision=highest
    )
    mixed = (within + carried_in + skip_gain[None, :, None] * values).reshape(
        tokens, heads_local * HEAD_DIM
    )
    gated = mixed * jax.nn.silu(gate_pre.astype(jnp.float32))
    group_width = heads_total * HEAD_DIM // GROUPS
    selector = (jnp.arange(GROUPS) == group_index).astype(jnp.float32)
    group_sums = lax.psum(jnp.sum(gated * gated, axis=1)[:, None] * selector[None, :], "tp")
    own_sum = jnp.sum(group_sums * selector[None, :], axis=1)
    normed = (gated * lax.rsqrt(own_sum / group_width + epsilon)[:, None] * gate_gain).astype(
        jnp.bfloat16
    )
    out_share = lax.psum_scatter(
        contract_columns(out_down, normed), "tp", scatter_dimension=0, tiled=True
    ).astype(jnp.bfloat16)
    update = contract_rows(lax.all_gather(out_share, "tp", axis=0, tiled=True), out_up)
    return (hidden_wide + update).astype(jnp.bfloat16)


def solution(mesh):
    return jax.shard_map(
        on_device,
        mesh=mesh,
        in_specs=(
            P("seq", "tp"),
            P("tp"),
            P("tp", None),
            P(None, "tp"),
            P(None, "tp"),
            P(None, "tp"),
            P(None, "tp"),
            P(None, "tp"),
            P(None, "tp"),
            P("tp"),
            P("tp"),
            P("tp"),
            P("tp"),
            P("tp", None),
            P(None, "tp"),
        ),
        out_specs=P("seq", "tp"),
        check_vma=False,
    )
```

profile of v0, /device:TPU:23, one launch (start us, length us, event | category | flops | bytes accessed | tf_op | source)
XLA Modules:
  0.0 305.5 jit_solution(9953234598632457863)
XLA Ops:
  6.5 4.6 %fusion.29 = f32[512,1024]{1,0:T(8,128)} fusion(bf16[1024,1024]{1,0:T(8,128)(2,1)} %param.19, bf16[512,1024]{1,0:T(8,128)(2,1)} %param.17, f32[1024]{0:T(1024)} %param.18), kind=kOutput, calls=%fused_computation.51 | convolution fusion | flops 1075314688 | bytes 5246976 | tf_op jit(solution)/shard_map/dot_general | solution.py:80
  11.3 1.1 copy-done.4
  12.4 0.3 fusion.20
  12.7 7.8 %psum.22 = f32[512]{0:T(512)S(1)} all-reduce(f32[512]{0:T(512)S(1)} %fusion.20), channel_id=1, replica_groups=mesh['seq'=8,'tp'=4] {'tp'}, use_global_device_ids=true, to_apply=%region_2.0 | all-reduce | flops 512 | bytes 4096 | tf_op jit(solution)/shard_map/psum | solution.py:81
  20.5 0.6 fusion.57
  21.1 76.4 %all-reduce.2.cloned.1.call-done = f32[512,1024]{1,0:T(8,128)} async-done(((f32[512,1024]{1,0:T(8,128)}), f32[512,1024]{1,0:T(8,128)}) %all-reduce.2.cloned.1.call-update) | async-done | bytes 2097168 | tf_op jit(solution)/shard_map/psum | solution.py:81
  97.5 1.8 multiply_convert_fusion.2
  99.3 0.4 fusion.28
  99.7 0.1 compare_select_fusion.1
  99.8 0.4 convolution_convert_fusion.2
  100.3 0.6 slice.90
  100.8 1.3 collective-permute-start.1
  102.1 1.2 reduce-window.6
  103.3 0.2 slice_reduce_fusion
  103.5 1.1 collective-permute-done.1
  104.6 0.7 maximum_convert_fusion.1
  105.3 1.7 multiply_convert_fusion.4
  107.1 2.8 convolution_convert_fusion.1
  110.0 1.3 collective-permute-start
  111.3 0.2 slice_reduce_fusion.1
  111.5 0.1 bitcast_exponential_fusion
  111.6 3.2 %collective-permute-done = bf16[3,1024]{1,0:T(4,128)(2,1)S(1)} collective-permute-done((bf16[3,1024]{1,0:T(4,128)(2,1)S(1)}, bf16[3,1024]{1,0:T(4,128)(2,1)S(1)}, u32[]{:S(2)}, u32[]{:S(2)}) %collective-permute-start) | collective-permute-done | bytes 6176 | tf_op jit(solution)/shard_map/ppermute | solution.py:18
  114.8 0.3 maximum_convert_fusion
  115.2 1.3 multiply_convert_fusion.1
  116.4 1.3 copy.29
  117.8 18.2 %all-gather.6.cloned.1.call-done = bf16[512,1024]{1,0:T(8,128)(2,1)} async-done(((bf16[512,256]{1,0:T(8,128)(2,1)}), bf16[512,1024]{1,0:T(8,128)(2,1)}) %all-gather.6.cloned.1.call-update) | async-done | bytes 1048592 | tf_op jit(solution)/shard_map/all_gather | solution.py:95
  136.0 3.2 %fusion.13 = f32[16,64,128]{2,1,0:T(8,128)} fusion(bf16[512,16,64]{0,2,1:T(8,128)(2,1)} %bitcast.86, f32[512,16]{0,1:T(8,128)S(1)} %get-tuple-element.63, bf16[512,1024]{1,0:T(8,128)(2,1)} %all-gather.6.cloned.1.call-done, s32[]{:T(128)S(6)} %select_n.35), kind=kOutput, calls=%fused_computation.22 | convolution fusion | flops 806354944 | bytes 1736708 | tf_op jit(solution)/shard_map/sh,shp,sn->hpn/dot_general | solution.py:116
  139.4 8.5 %all-gather.1 = f32[8,1,16]{2,1,0:T(1,128)S(1)} all-gather(f32[1,1,16]{2,1,0:T(1,128)S(1)} %bitcast.100), channel_id=1, replica_groups=mesh['seq'=8,'tp'=4] {'seq'}, dimensions={0}, use_global_device_ids=true | all-gather | bytes 576 | tf_op jit(solution)/shard_map/all_gather | solution.py:23
  147.9 2.3 fusion.42
  150.2 26.4 %all-gather.10.cloned.1.call-done = f32[128,64,128]{2,1,0:T(8,128)} async-done(((f32[16,64,128]{2,1,0:T(8,128)}), f32[128,64,128]{2,1,0:T(8,128)}) %all-gather.10.cloned.1.call-update) | async-done | bytes 4194320 | tf_op jit(solution)/shard_map/all_gather | solution.py:23
  176.6 8.8 %while.12 = (s32[]{:T(128)}, f32[16,64,128]{2,1,0:T(8,128)S(1)}, s32[]{:T(128)}, f32[8,16]{1,0:T(8,128)S(1)}, f32[8,16,64,128]{3,2,1,0:T(8,128)}, /*index=5*/s32[]{:T(128)}, s32[]{:T(128)}, s32[]{:T(128)}) while((s32[]{:T(128)}, f32[16,64,128]{2,1,0:T(8,128)S(1)}, s32[]{:T(128)}, f32[8,16]{1,0:T(8,128)S(1)}, f32[8,16,64,128]{3,2,1,0:T(8,128)}, ...), condition=%wide.region_6.7_spmd, body=%wide.region_5.6_spmd.sunk | while | flops 262149 | bytes 1573183 | solution.py:31
  176.7 1.2 bitcast_add_fusion.3
  177.9 1.2 bitcast_add_fusion.3
  179.2 1.2 bitcast_add_fusion.3
  180.4 1.2 bitcast_add_fusion.3
  181.6 1.2 bitcast_add_fusion.3
  182.9 1.2 bitcast_add_fusion.3
  184.1 1.2 bitcast_add_fusion.3
  185.5 2.0 fusion.39
  187.6 14.3 %fusion.14 = f32[512,16,64]{0,2,1:T(8,128)} fusion(bf16[512,16,64]{0,2,1:T(8,128)(2,1)S(1)} %bitcast.87, f32[512,16,64]{0,2,1:T(8,128)S(1)} %fusion.39, f32[16,512]{1,0:T(8,128)S(1)} %get-tuple-element.66, f32[16,512]{1,0:T(8,128)S(1)} %get-tuple-element.64, f32[512,512]{1,0:T(8,128)S(1)} %copy-done.6, pred[512,512]{1,0:T(8,128)(4,1)S(1)} %iota_compare_fusion, ...), kind=kOutput, calls=%fused_computation.23 | convolution fusion | flops 3244818432 | bytes 6651968 | tf_op jit(solution)/shard_map/hts,shp->thp/dot_general | solution.py:114
  201.9 3.0 copy.32
  204.9 4.5 %multiply_reduce_fusion = (f32[512]{0:T(512)S(1)}, f32[512,1024]{1,0:T(8,128)}) fusion(f32[512,1024]{1,0:T(8,128)} %copy.32, bf16[512,1024]{1,0:T(8,128)(2,1)S(1)} %copy-done.3, bf16[1024,1024]{1,0:T(8,128)(2,1)S(1)} %copy-done), kind=kOutput, calls=%fused_computation.40 | convolution fusion | flops 1078459904 | bytes 7342080 | tf_op jit(solution)/shard_map/dot_general | solution.py:85
  209.5 7.0 %psum.23 = f32[512,4]{0,1:T(4,128)S(1)} all-reduce(f32[512,4]{0,1:T(4,128)S(1)} %broadcast_multiply_fusion), channel_id=1, replica_groups=mesh['seq'=8,'tp'=4] {'tp'}, use_global_device_ids=true, to_apply=%region_8.9 | all-reduce | flops 2048 | bytes 16384 | tf_op jit(solution)/shard_map/psum | solution.py:138
  216.6 4.8 %convolution_bitcast_fusion = f32[1024,512]{0,1:T(8,128)} fusion(bf16[1024,1024]{1,0:T(8,128)(2,1)} %param.30, f32[512,1024]{1,0:T(8,128)} %get-tuple-element.77, f32[1024]{0:T(1024)S(1)} %copy-done.12, f32[512]{0:T(512)S(1)} %add_rsqrt_fusion), kind=kOutput, calls=%fused_computation.43 | convolution fusion | flops 1075314688 | bytes 6297600 | tf_op jit(solution)/shard_map/dot_general | solution.py:41
  221.5 44.2 %reduce-scatter.2.cloned.1.call-done = f32[256,512]{0,1:T(8,128)} async-done(((f32[1024,512]{0,1:T(8,128)}), f32[256,512]{0,1:T(8,128)}) %reduce-scatter.2.cloned.1.call-update) | async-done | bytes 524304 | tf_op jit(solution)/shard_map/reduce_scatter | solution.py:143
  265.7 1.8 convert_element_type.79
  267.5 27.4 %all-gather.8.cloned.1.call-done = bf16[1024,512]{0,1:T(8,128)(2,1)} async-done(((bf16[256,512]{0,1:T(8,128)(2,1)}), bf16[1024,512]{0,1:T(8,128)(2,1)}) %all-gather.8.cloned.1.call-update) | async-done | bytes 1048592 | tf_op jit(solution)/shard_map/all_gather | solution.py:146
  294.9 4.1 %fusion.21 = bf16[512,1024]{1,0:T(8,128)(2,1)} fusion(bf16[512,1024]{1,0:T(8,128)(2,1)S(1)} %copy-done.5, bf16[1024,512]{0,1:T(8,128)(2,1)} %all-gather.8.cloned.1.call-done, bf16[1024,1024]{1,0:T(8,128)(2,1)} %param.31), kind=kOutput, calls=%fused_computation.30 | convolution fusion | flops 1075314688 | bytes 5242880 | tf_op jit(solution)/shard_map/dot_general | solution.py:35
  (60 shorter events, 0.8 us)
Async XLA Ops:
  6.5 198.4 %copy-start = (bf16[1024,1024]{1,0:T(8,128)(2,1)S(1)}, bf16[1024,1024]{1,0:T(8,128)(2,1)}, u32[]{:S(2)}) copy-start(bf16[1024,1024]{1,0:T(8,128)(2,1)} %param.20) | copy-start | bytes 6291460
  6.5 90.9 %all-reduce.2.cloned.1.call-start = ((), (), s32[]{:S(2)}) async-start(), calls=%async_computation.1 | async-start | bytes 4194304 | tf_op jit(solution)/shard_map/psum | solution.py:81
  11.2 1.2 copy-start.4
  11.2 9.3 %copy-start.13 = (f32[16]{0:T(128)S(1)}, f32[16]{0:T(128)}, u32[]{:S(2)}) copy-start(f32[16]{0:T(128)} %param.27) | copy-start | bytes 196
  11.2 9.3 %copy-start.9 = (f32[4,256]{1,0:T(4,128)S(1)}, f32[4,256]{1,0:T(4,128)}, u32[]{:S(2)}) copy-start(f32[4,256]{1,0:T(4,128)} %param.25) | copy-start | bytes 12292
  11.2 9.9 %copy-start.8 = (f32[4,1024]{1,0:T(4,128)S(1)}, f32[4,1024]{1,0:T(4,128)}, u32[]{:S(2)}) copy-start(f32[4,1024]{1,0:T(4,128)} %param.24) | copy-start | bytes 49156
  11.2 124.8 %all-gather.6.cloned.1.call-start = ((), (), s32[]{:S(2)}) async-start(), calls=%async_computation.2 | async-start | bytes 1310720 | tf_op jit(solution)/shard_map/all_gather | solution.py:95
  12.4 86.9 %copy-start.7 = (bf16[1024,16]{0,1:T(8,128)(2,1)S(1)}, bf16[1024,16]{0,1:T(8,128)(2,1)}, u32[]{:S(2)}) copy-start(bf16[1024,16]{0,1:T(8,128)(2,1)} %param.23) | copy-start | bytes 98308
  12.4 86.9 %copy-start.10 = (f32[16]{0:T(128)S(1)}, f32[16]{0:T(128)}, u32[]{:S(2)}) copy-start(f32[16]{0:T(128)} %param.26) | copy-start | bytes 196
  97.5 2.3 copy-start.11
  99.3 7.8 %copy-start.2 = (bf16[512,1024]{1,0:T(8,128)(2,1)}, bf16[512,1024]{1,0:T(8,128)(2,1)S(1)}, u32[]{:S(2)}) copy-start(bf16[512,1024]{1,0:T(8,128)(2,1)S(1)} %multiply_convert_fusion.2) | copy-start | bytes 3145732
  100.8 3.7 %collective-permute-start.1 = (bf16[3,256]{1,0:T(4,128)(2,1)}, bf16[3,256]{1,0:T(4,128)(2,1)}, u32[]{:S(2)}, u32[]{:S(2)}) collective-permute-start(bf16[3,256]{1,0:T(4,128)(2,1)} %slice.90), channel_id=1, source_target_pairs={{0,4},{4,8},{8,12},{12,16},{16,20},{20,24},{24,28},{1,5},{5,9},{9,... | collective-permute-start | bytes 4616 | tf_op jit(solution)/shard_map/ppermute | solution.py:18
  107.0 69.5 %all-gather.10.cloned.1.call-start = ((), (), s32[]{:S(2)}) async-start(), calls=%async_computation.5 | async-start | bytes 4718592 | tf_op jit(solution)/shard_map/all_gather | solution.py:23
  110.0 4.9 %collective-permute-start = (bf16[3,1024]{1,0:T(4,128)(2,1)S(1)}, bf16[3,1024]{1,0:T(4,128)(2,1)S(1)}, u32[]{:S(2)}, u32[]{:S(2)}) collective-permute-start(bf16[3,1024]{1,0:T(4,128)(2,1)S(1)} %slice.85), channel_id=1, source_target_pairs={{0,4},{4,8},{8,12},{12,16},{16,20},{20,24},{24,28},{1,5},{5,9},{9,... | collective-permute-start | bytes 18440 | tf_op jit(solution)/shard_map/ppermute | solution.py:18
  139.2 126.5 %reduce-scatter.2.cloned.1.call-start = ((), (), s32[]{:S(2)}) async-start(), calls=%async_computation.3 | async-start | bytes 2621440 | tf_op jit(solution)/shard_map/reduce_scatter | solution.py:143
  185.5 2.1 copy-start.1
  185.5 2.1 copy-start.6
  185.5 2.1 copy-start.14
  201.9 3.0 copy-start.3
  204.9 11.6 %copy-start.12 = (f32[1024]{0:T(1024)S(1)}, f32[1024]{0:T(1024)}, u32[]{:S(2)}) copy-start(f32[1024]{0:T(1024)} %param.29) | copy-start | bytes 12292
  221.4 73.5 %copy-start.5 = (bf16[512,1024]{1,0:T(8,128)(2,1)S(1)}, bf16[512,1024]{1,0:T(8,128)(2,1)}, u32[]{:S(2)}) copy-start(bf16[512,1024]{1,0:T(8,128)(2,1)} %param.17) | copy-start | bytes 3145732
  221.4 73.4 %all-gather.8.cloned.1.call-start = ((), (), s32[]{:S(2)}) async-start(), calls=%async_computation.4 | async-start | bytes 1310720 | tf_op jit(solution)/shard_map/all_gather | solution.py:146
Sparse Core Ops, SparseCore 0:
  11.3 86.1 all-reduce.1
  107.2 28.7 all-gather.5
  139.3 37.2 all-gather.9
  221.5 44.1 reduce-scatter.1
  267.6 27.1 all-gather.7
where the time goes:
time: 311 us; the launch traced here: 306 us
  waiting for transfers between devices  197 us (63%)
  matrix products  43.6 us (14%)
  blocking collectives  23.3 us (7%)
  other arithmetic  17.9 us (6%)
  between operations  13.4 us (4%)
  local copies, waits for them, and re-layouts  7.19 us (2%)
    psum x1, waiting for transfers between devices, on_device(): summed, total_squares = lax.psum((partial_value, local_squares), 'tp')  76.4 us
    reduce_scatter x1, waiting for transfers between devices, on_device(): lax.psum_scatter(contract_columns(out_down, normed), 'tp', scatter_dimens...  44.2 us
    all_gather x1, waiting for transfers between devices, on_device(): lax.all_gather(out_share, 'tp', axis=0, tiled=True)  27.4 us
    all_gather x1, waiting for transfers between devices, entering(): gathered = jax.tree.map(lambda a: lax.all_gather(a, axis), part)  26.4 us
    all_gather x1, waiting for transfers between devices, on_device(): state_all = lax.all_gather(state_act, 'tp', axis=1, tiled=True)  18.2 us
    dot_general x1, matrix products, on_device(): within = jnp.einsum('hts,shp->thp', mixing, values, precision=highest)  14.3 us
    all_gather x1, blocking collectives, entering(): gathered = jax.tree.map(lambda a: lax.all_gather(a, axis), part)  8.52 us
    add x7, other arithmetic, combine(): later[0][:, None, None] * earlier[1] + later[1]  8.31 us
  transfers between devices with their start and end apart: 7, of which 7 were waited for; matrix products, arithmetic and copies ran while one was open for 4% of the time, Pallas kernels for 0%

commit v1 on v0

v1 whole, which is shorter than its diff:
```python
import functools

import jax
import jax.numpy as jnp
from jax import lax
from jax.experimental import pallas as pl
from jax.experimental.pallas import tpu as pltpu
from jax.sharding import PartitionSpec as P

HEAD_DIM = 64
NSTATE = 128
GROUPS = 4

epsilon = 1e-05
MESH = pl.DeviceIdType.MESH
VMEM_LIMIT = 56 * 1024 * 1024


def greet(axis, offsets):
    count = lax.axis_size(axis)
    me = lax.axis_index(axis)
    barrier = pltpu.get_barrier_semaphore()
    for offset in offsets:
        pl.semaphore_signal(
            barrier, inc=1, device_id={axis: lax.rem(me + offset, count)}, device_id_type=MESH
        )
    pl.semaphore_wait(barrier, len(offsets))


def send(source, target, send_sem, recv_sem, axis, peer):
    copy = pltpu.make_async_remote_copy(
        src_ref=source,
        dst_ref=target,
        send_sem=send_sem,
        recv_sem=recv_sem,
        device_id={axis: peer},
        device_id_type=MESH,
    )
    copy.start()
    return copy


def project_kernel(
    n, with_norm, width, *refs
):
    if with_norm:
        (rows_ref, gain_ref, weight_ref, out_ref, parts, arrived, own, sq_parts, sq_arrived,
         part_send, part_recv, sq_send, sq_recv, full_send, full_recv) = refs
    else:
        (rows_ref, weight_ref, out_ref, parts, arrived, own,
         part_send, part_recv, full_send, full_recv) = refs
    me = lax.axis_index("tp")
    length = rows_ref.shape[0] // n
    greet("tp", range(1, n))
    copies = []
    own_squares = None
    order = [o for o in sorted(range(1, n), key=lambda o: -min(o, n - o))] + [0]
    for offset in order:
        peer = lax.rem(me + offset, n)
        start = pl.multiple_of(peer * length, length)
        rows = rows_ref[pl.ds(start, length), :]
        if with_norm:
            wide = rows.astype(jnp.float32)
            squares = jnp.sum(wide * wide, axis=1, keepdims=True)
            rows = (wide * gain_ref[...]).astype(jnp.bfloat16)
            if offset:
                spread = jnp.broadcast_to(squares, (length, 128))
                sq_parts[offset - 1] = spread.T[:8]
                copies.append(
                    send(sq_parts.at[offset - 1], sq_arrived.at[offset - 1],
                         sq_send.at[offset - 1], sq_recv.at[offset - 1], "tp", peer)
                )
            else:
                own_squares = squares
        part = jnp.dot(rows, weight_ref[...], preferred_element_type=jnp.float32)
        if offset:
            parts[offset - 1] = part.astype(jnp.bfloat16)
            copies.append(
                send(parts.at[offset - 1], arrived.at[offset - 1],
                     part_send.at[offset - 1], part_recv.at[offset - 1], "tp", peer)
            )
        else:
            own[...] = part
    for copy in copies:
        copy.wait_recv()
    total = own[...]
    for offset in range(1, n):
        total = total + arrived[offset - 1].astype(jnp.float32)
    if with_norm:
        others = sq_arrived[0]
        for offset in range(2, n):
            others = others + sq_arrived[offset - 1]
        column = jnp.broadcast_to(others[:1], (128, length)).T[:, :1]
        factor = lax.rsqrt((own_squares + column) / width + epsilon)
        total = total * factor
    mine = pl.multiple_of(me * length, length)
    out_ref[pl.ds(mine, length), :] = total.astype(jnp.bfloat16)
    full = [
        send(out_ref.at[pl.ds(mine, length), :], out_ref.at[pl.ds(mine, length), :],
             full_send.at[offset - 1], full_recv.at[offset - 1], "tp", lax.rem(me + offset, n))
        for offset in order[:-1]
    ]
    for copy in full:
        copy.wait_recv()
    for copy in copies + full:
        copy.wait_send()


def project(rows, weight, gain, width, collective_id):
    n = lax.axis_size("tp")
    tokens = rows.shape[0]
    length, rank = tokens // n, weight.shape[1]
    vmem = pl.BlockSpec(memory_space=pltpu.VMEM)
    sems = pltpu.SemaphoreType.DMA((n - 1,))
    with_norm = gain is not None
    scratch = [
        pltpu.VMEM((n - 1, length, rank), jnp.bfloat16),
        pltpu.VMEM((n - 1, length, rank), jnp.bfloat16),
        pltpu.VMEM((length, rank), jnp.float32),
    ]
    if with_norm:
        scratch += [pltpu.VMEM((n - 1, 8, length), jnp.float32)] * 2
    scratch += [sems] * (6 if with_norm else 4)
    operands = (rows, gain[None], weight) if with_norm else (rows, weight)
    return pl.pallas_call(
        functools.partial(project_kernel, n, with_norm, width),
        out_shape=jax.ShapeDtypeStruct((tokens, rank), jnp.bfloat16),
        in_specs=[vmem] * len(operands),
        out_specs=vmem,
        scratch_shapes=scratch,
        compiler_params=pltpu.CompilerParams(
            collective_id=collective_id, has_side_effects=True, vmem_limit_bytes=VMEM_LIMIT
        ),
    )(*operands)


def exchange_kernel(n, share, act_ref, out_ref, sends, recvs, local_sem):
    me = lax.axis_index("tp")
    columns = act_ref.shape[1]
    piece = out_ref.shape[2]
    pieces, slots = columns // piece, out_ref.shape[0]
    greet("tp", range(1, n))

    def place(index):
        column = index * piece
        side = column // (GROUPS * NSTATE)
        within = column - side * (GROUPS * NSTATE)
        group = within // NSTATE
        slot = side * (NSTATE // piece) + (within - group * NSTATE) // piece
        return group, slot

    def remote(k, r, target, slot):
        return pltpu.make_async_remote_copy(
            src_ref=act_ref.at[:, pl.ds(k * piece, piece)],
            dst_ref=out_ref.at[slot],
            send_sem=sends.at[k * share + r],
            recv_sem=recvs.at[slot],
            device_id={"tp": target},
            device_id_type=MESH,
        )

    for k in range(pieces):
        group, slot = place(me * pieces + k)
        for r in range(share):
            target = group * share + r

            @pl.when(target != me)
            def _():
                remote(k, r, target, slot).start()

            @pl.when(target == me)
            def _():
                local = pltpu.make_async_copy(
                    act_ref.at[:, pl.ds(k * piece, piece)], out_ref.at[slot], local_sem
                )
                local.start()
                local.wait()

    mine = me // share
    per_side = NSTATE // piece
    for slot in range(slots):
        side = slot // per_side
        source = (side * GROUPS * per_side + mine * per_side + slot % per_side) // pieces

        @pl.when(source != me)
        def _():
            remote(0, 0, me, slot).wait_recv()

    for k in range(pieces):
        group, slot = place(me * pieces + k)
        for r in range(share):

            @pl.when(group * share + r != me)
            def _():
                remote(k, r, group * share + r, slot).wait_send()


def exchange(act, collective_id):
    n = lax.axis_size("tp")
    tokens, columns = act.shape
    piece = min(columns, NSTATE)
    share = n // GROUPS
    slots = 2 * NSTATE // piece
    vmem = pl.BlockSpec(memory_space=pltpu.VMEM)
    return pl.pallas_call(
        functools.partial(exchange_kernel, n, share),
        out_shape=jax.ShapeDtypeStruct((slots, tokens, piece), act.dtype),
        in_specs=[vmem],
        out_specs=vmem,
        scratch_shapes=[
            pltpu.SemaphoreType.DMA((columns // piece * share,)),
            pltpu.SemaphoreType.DMA((slots,)),
            pltpu.SemaphoreType.DMA,
        ],
        compiler_params=pltpu.CompilerParams(
            collective_id=collective_id, has_side_effects=True, vmem_limit_bytes=VMEM_LIMIT
        ),
    )(act)


def shifted(shard, axis, by):
    peers = lax.axis_size(axis)
    pairs = [(i, i + by) for i in range(peers) if 0 <= i + by < peers]
    return lax.ppermute(shard, axis, pairs)


def entering(part, axis, combine, identity):
    place = lax.axis_index(axis)
    gathered = jax.tree.map(lambda a: lax.all_gather(a, axis), part)
    state = jax.tree.map(lambda a, e: jnp.zeros_like(a) + jnp.asarray(e, a.dtype), part, identity)

    def one(lap, state):
        return combine(
            state, jax.tree.map(lambda a: lax.dynamic_index_in_dim(a, lap, 0, False), gathered)
        )

    return lax.fori_loop(0, place, one, state)


def depthwise(rim_rows, current, weights):
    joined = jnp.concatenate([rim_rows, current], axis=0).astype(jnp.float32)
    length = current.shape[0]
    result = jnp.zeros(current.shape, jnp.float32)
    for offset in range(weights.shape[0]):
        result = result + weights[offset] * joined[offset : offset + length]
    return jax.nn.silu(result).astype(jnp.bfloat16)


def on_device(
    hidden,
    norm_gain,
    rank_down,
    gate_up,
    value_up,
    state_up,
    step_up,
    conv_value,
    conv_state,
    step_bias,
    decay_log,
    skip_gain,
    gate_gain,
    out_down,
    out_up,
):
    tokens = hidden.shape[0]
    tp_count = lax.axis_size("tp")
    tp_index = lax.axis_index("tp")
    model_width = hidden.shape[1] * tp_count
    up_weights = (gate_up, value_up, state_up, step_up)
    reduced = project(hidden, rank_down, norm_gain, model_width, 0)
    projected = tuple(
        (jnp.dot(reduced, weight, preferred_element_type=jnp.float32) for weight in up_weights)
    )
    gate_pre = projected[0].astype(jnp.bfloat16)
    value_pre = projected[1].astype(jnp.bfloat16)
    state_pre = projected[2].astype(jnp.bfloat16)
    step_pre = projected[3].astype(jnp.bfloat16)
    rim_start = tokens - conv_value.shape[0] + 1
    rim_value, rim_state = shifted((value_pre[rim_start:], state_pre[rim_start:]), "seq", 1)
    value_act = depthwise(rim_value, value_pre, conv_value)
    state_act = depthwise(rim_state, state_pre, conv_state)
    heads_local = decay_log.shape[0]
    heads_total = heads_local * tp_count
    group_index = tp_index * heads_local // (heads_total // GROUPS)
    sides = exchange(state_act, 1)
    half = sides.shape[0] // 2
    inward = jnp.concatenate([sides[i] for i in range(half)], axis=1)
    outward = jnp.concatenate([sides[half + i] for i in range(half)], axis=1)
    step_size = jax.nn.softplus(step_pre.astype(jnp.float32) + step_bias)
    log_decay = jnp.cumsum(-jnp.exp(decay_log) * step_size, axis=0)
    values = value_act.astype(jnp.float32).reshape(tokens, heads_local, HEAD_DIM)
    coupling = lax.dot_general(
        outward, inward, (((1,), (1,)), ((), ())), preferred_element_type=jnp.float32
    )
    positions = jnp.arange(tokens)
    causal = positions[:, None] >= positions[None, :]
    spread = log_decay.T[:, :, None] - log_decay.T[:, None, :]
    attenuation = jnp.where(causal[None], jnp.exp(jnp.where(causal[None], spread, 0.0)), 0.0)
    mixing = coupling[None] * attenuation * step_size.T[:, None, :]
    narrow_values = value_act.reshape(tokens, heads_local, HEAD_DIM)
    within = jnp.einsum(
        "hts,shp->thp",
        mixing.astype(jnp.bfloat16),
        narrow_values,
        preferred_element_type=jnp.float32,
    )
    ending = jnp.exp(log_decay[-1][None, :] - log_decay) * step_size
    weighted = (ending[:, :, None] * values).astype(jnp.bfloat16)
    local_state = jnp.einsum("shp,sn->hpn", weighted, inward, preferred_element_type=jnp.float32)
    local_decay = jnp.exp(log_decay[-1])

    def combine(earlier, later):
        return (earlier[0] * later[0], later[0][:, None, None] * earlier[1] + later[1])

    prefix = entering(
        (local_decay, local_state),
        "seq",
        combine,
        (jnp.ones_like(local_decay), jnp.zeros_like(local_state)),
    )
    incoming = prefix[1]
    carried_in = jnp.exp(log_decay)[:, :, None] * jnp.einsum(
        "tn,hpn->thp",
        outward,
        incoming.astype(jnp.bfloat16),
        preferred_element_type=jnp.float32,
    )
    mixed = (within + carried_in + skip_gain[None, :, None] * values).reshape(
        tokens, heads_local * HEAD_DIM
    )
    gated = mixed * jax.nn.silu(gate_pre.astype(jnp.float32))
    group_width = heads_total * HEAD_DIM // GROUPS
    own_sum = jnp.sum(gated * gated, axis=1)
    if heads_local * HEAD_DIM < group_width:
        selector = (jnp.arange(GROUPS) == group_index).astype(jnp.float32)
        group_sums = lax.psum(own_sum[:, None] * selector[None, :], "tp")
        own_sum = jnp.sum(group_sums * selector[None, :], axis=1)
    normed = (gated * lax.rsqrt(own_sum / group_width + epsilon)[:, None] * gate_gain).astype(
        jnp.bfloat16
    )
    shared = project(normed, out_down, None, None, 2)
    update = jnp.dot(shared, out_up, preferred_element_type=jnp.float32)
    return (hidden.astype(jnp.float32) + update).astype(jnp.bfloat16)


def solution(mesh):
    return jax.shard_map(
        on_device,
        mesh=mesh,
        in_specs=(
            P("seq", "tp"),
            P("tp"),
            P("tp", None),
            P(None, "tp"),
            P(None, "tp"),
            P(None, "tp"),
            P(None, "tp"),
            P(None, "tp"),
            P(None, "tp"),
            P("tp"),
            P("tp"),
            P("tp"),
            P("tp"),
            P("tp", None),
            P(None, "tp"),
        ),
        out_specs=P("seq", "tp"),
        check_vma=False,
    )
```

time: 311 us -> 229 us (0.74); the launches traced: 306 us -> 228 us
  waiting for transfers between devices: 197 us -> 24.7 us
  Pallas kernels: 0 us -> 116 us
  matrix products: 43.6 us -> 23.1 us
  blocking collectives: 23.3 us -> 13.1 us
  local copies, waits for them, and re-layouts: 7.19 us -> 17 us
    pallas_call x0 -> x3, Pallas kernels: none -> 116 us  [the longest x2 110 us: project(): pl.pallas_call(functools.partial(project_kernel, n, with_norm, width), ou...]
    psum x1 -> x0, waiting for transfers between devices: 76.4 us -> none  [on_device(): summed, total_squares = lax.psum((partial_value, local_squares), 'tp')]
    all_gather x2 -> x0, waiting for transfers between devices: 45.6 us -> none  [the longest x1 27.4 us: on_device(): lax.all_gather(out_share, 'tp', axis=0, tiled=True)]
    reduce_scatter x1 -> x0, waiting for transfers between devices: 44.2 us -> none  [on_device(): lax.psum_scatter(contract_columns(out_down, normed), 'tp', scatter_dimens...]
    dot_general x7 -> x5, matrix products: 35.4 us -> 16.5 us  [the longest x1 8.8 us: on_device(): jnp.einsum('hts,shp->thp', mixing.astype(jnp.bfloat16), narrow_values, pr...]
    psum x2 -> x0, blocking collectives: 14.7 us -> none  [the longest x1 7.77 us: on_device(): summed, total_squares = lax.psum((partial_value, local_squares), 'tp')]
    all_gather x1, blocking collectives: 8.52 us -> 13.1 us  [entering(): gathered = jax.tree.map(lambda a: lax.all_gather(a, axis), part)]
    mul x0 -> x2, local copies, waits for them, and re-layouts: none -> 4.48 us  [on_device(): weighted = (ending[:, :, None] * values).astype(jnp.bfloat16)]
  transfers between devices with their start and end apart: 7 -> 3, of which waited for: 7 -> 1; matrix products, arithmetic and copies ran while one was open for 4% -> 7% of each run, Pallas kernels for 0% -> 3%
where the time goes in v1:
time: 229 us; the launch traced here: 228 us
  Pallas kernels  116 us (51%)
  waiting for transfers between devices  24.7 us (11%)
  matrix products  23.1 us (10%)
  other arithmetic  17.5 us (8%)
  local copies, waits for them, and re-layouts  17 us (7%)
  between operations  13.7 us (6%)
  blocking collectives  13.1 us (6%)
  starting transfers between devices  2.56 us (1%)
    pallas_call x2, Pallas kernels, project(): pl.pallas_call(functools.partial(project_kernel, n, with_norm, width), ou...  110 us
    all_gather x1, waiting for transfers between devices, entering(): gathered = jax.tree.map(lambda a: lax.all_gather(a, axis), part)  24.6 us
    all_gather x1, blocking collectives, entering(): gathered = jax.tree.map(lambda a: lax.all_gather(a, axis), part)  13.1 us
    dot_general x1, matrix products, on_device(): jnp.einsum('hts,shp->thp', mixing.astype(jnp.bfloat16), narrow_values, pr...  8.8 us
    add x7, other arithmetic, combine(): later[0][:, None, None] * earlier[1] + later[1]  8.31 us
    dot_general x4, matrix products, on_device(): jnp.dot(reduced, weight, preferred_element_type=jnp.float32)  6.65 us
    pallas_call x1, Pallas kernels, exchange(): pl.pallas_call(functools.partial(exchange_kernel, n, share), out_shape=ja...  6.03 us
  transfers between devices with their start and end apart: 3, of which 1 were waited for; matrix products, arithmetic and copies ran while one was open for 7% of the time, Pallas kernels for 3%

profile of v1, /device:TPU:23, one launch (start us, length us, event | category | flops | bytes accessed | tf_op | source)
XLA Modules:
  0.0 228.3 jit_solution(2928219978858996554)
XLA Ops:
  6.5 55.4 %shard_map.145 = bf16[512,1024]{1,0:T(8,128)(2,1)} custom-call(bf16[512,1024]{1,0:T(8,128)(2,1)} %refs_0_.1, f32[1,1024]{1,0:T(1,128)} %bitcast.103, bf16[1024,1024]{1,0:T(8,128)(2,1)} %refs_2_.1), custom_call_target="tpu_custom_call" | custom-call | tf_op jit(solution)/shard_map/pallas_call | solution.py:125
  62.0 0.0 copy-start.16
  62.0 2.6 %convolution_convert_fusion.1 = bf16[512,1024]{1,0:T(8,128)(2,1)S(1)} fusion(bf16[512,1024]{1,0:T(8,128)(2,1)} %shard_map.145, bf16[1024,1024]{1,0:T(8,128)(2,1)S(1)} %copy-done.14), kind=kOutput, calls=%fused_computation.26 | convolution fusion | flops 1074266112 | bytes 4194304 | tf_op jit(solution)/shard_map/dot_general | solution.py:273
  64.6 0.6 slice.93
  65.2 1.3 collective-permute-start
  66.6 0.4 convolution_convert_fusion.2
  67.0 0.6 slice.98
  67.6 1.3 collective-permute-start.1
  68.9 0.4 fusion.11
  69.3 0.1 compare_select_fusion.1
  69.4 1.1 reduce-window.6
  70.5 0.2 slice_reduce_fusion
  70.7 0.1 copy_bitcast_fusion
  70.8 0.7 slice_reduce_fusion.1
  71.5 0.7 bitcast_exponential_fusion
  72.2 0.8 fusion.35
  73.1 1.6 mul.217
  74.7 2.9 %copy.33 = f32[512,1024]{1,0:T(8,128)} copy(f32[512,1024]{0,1:T(8,128)} %bitcast.92) | data formatting | bytes 4194304 | tf_op jit(solution)/shard_map/mul | solution.py:309
  77.6 0.7 maximum_convert_fusion.1
  78.3 1.0 multiply_convert_fusion.7.act_ref
  79.3 6.0 %shard_map.146 = bf16[2,512,128]{2,1,0:T(8,128)(2,1)} custom-call(bf16[512,256]{1,0:T(8,128)(2,1)} %multiply_convert_fusion.7.act_ref), custom_call_target="tpu_custom_call" | custom-call | tf_op jit(solution)/shard_map/pallas_call | solution.py:205
  85.4 1.0 maximum_convert_fusion
  86.4 2.3 %multiply_convert_fusion.3 = (bf16[512,1024]{1,0:T(8,128)(2,1)}, bf16[512,1024]{1,0:T(8,128)(2,1)S(1)}) fusion(f32[512,1024]{1,0:T(8,128)S(1)} %copy-done.1, f32[515,1024]{1,0:T(8,128)S(1)} %maximum_convert_fusion, f32[1024]{0:T(1024)S(1)} %bitcast.101, f32[1024]{0:T(1024)S(1)} %bitcast.102, f32[1024]{0:T(1024)S(1)} %bitcast.100, f32[1024]{0:T(1024)S(1)} %bitcast.99), kind=kLoop, calls=%fused_computation.23 | loop fusion | flops 7864320 | bytes 12599296 | tf_op jit(solution)/shard_map/convert_element_type | solution.py:309
  88.7 2.3 %copy.34 = bf16[512,1024]{0,1:T(8,128)(2,1)} copy(bf16[512,1024]{1,0:T(8,128)(2,1)} %get-tuple-element.62) | data formatting | bytes 2097152 | tf_op jit(solution)/shard_map/convert_element_type | solution.py:309
  91.0 2.5 %fusion.17 = f32[16,64,128]{2,1,0:T(8,128)} fusion(bf16[512,16,64]{0,2,1:T(8,128)(2,1)} %bitcast.93, bf16[2,512,128]{2,1,0:T(8,128)(2,1)S(1)} %copy-done.4), kind=kOutput, calls=%fused_computation.44 | convolution fusion | flops 134217728 | bytes 1703936 | tf_op jit(solution)/shard_map/shp,sn->hpn/dot_general | solution.py:310
  93.5 0.0 all-gather.4.cloned.1.call-update
  93.6 13.1 %all-gather.1 = f32[8,1,16]{2,1,0:T(1,128)S(1)} all-gather(f32[1,1,16]{2,1,0:T(1,128)S(1)} %bitcast.109), channel_id=1, replica_groups=mesh['seq'=8,'tp'=4] {'seq'}, dimensions={0}, use_global_device_ids=true | all-gather | bytes 576 | tf_op jit(solution)/shard_map/all_gather | solution.py:229
  106.7 0.8 iota_compare_fusion
  107.5 1.3 fusion.20
  108.8 1.6 copy.35
  110.5 1.3 copy.30
  111.8 24.6 %all-gather.4.cloned.1.call-done = f32[128,64,128]{2,1,0:T(8,128)} async-done(((f32[16,64,128]{2,1,0:T(8,128)}), f32[128,64,128]{2,1,0:T(8,128)}) %all-gather.4.cloned.1.call-update) | async-done | bytes 4194320 | tf_op jit(solution)/shard_map/all_gather | solution.py:229
  136.5 8.8 %while.12 = (s32[]{:T(128)}, f32[16,64,128]{2,1,0:T(8,128)S(1)}, s32[]{:T(128)}, f32[8,16]{1,0:T(8,128)S(1)}, f32[8,16,64,128]{3,2,1,0:T(8,128)}, /*index=5*/s32[]{:T(128)}, s32[]{:T(128)}, s32[]{:T(128)}) while((s32[]{:T(128)}, f32[16,64,128]{2,1,0:T(8,128)S(1)}, s32[]{:T(128)}, f32[8,16]{1,0:T(8,128)S(1)}, f32[8,16,64,128]{3,2,1,0:T(8,128)}, ...), condition=%wide.region_3.4_spmd, body=%wide.region_2.3_spmd.sunk | while | flops 262149 | bytes 1573183 | solution.py:237
  136.5 1.2 bitcast_add_fusion.3
  137.8 1.2 bitcast_add_fusion.3
  139.0 1.2 bitcast_add_fusion.3
  140.3 1.2 bitcast_add_fusion.3
  141.5 1.2 bitcast_add_fusion.3
  142.7 1.2 bitcast_add_fusion.3
  144.0 1.2 bitcast_add_fusion.3
  145.4 0.4 fusion.15
  145.8 1.1 copy-done.5
  147.0 8.8 %fusion.9 = f32[512,16,64]{0,2,1:T(8,128)} fusion(f32[512,16,64]{0,2,1:T(8,128)S(1)} %bitcast.94, f32[512,16,64]{0,2,1:T(8,128)S(1)} %fusion.15, bf16[512,16,64]{0,2,1:T(8,128)(2,1)} %bitcast.97, f32[16,512]{1,0:T(8,128)S(1)} %get-tuple-element.68, f32[16,512]{1,0:T(8,128)S(1)} %get-tuple-element.66, f32[512,512]{1,0:T(8,128)} %fusion.20, ...), kind=kOutput, calls=%fused_computation.19 | convolution fusion | flops 564133888 | bytes 8749120 | tf_op jit(solution)/shard_map/hts,shp->thp/dot_general | solution.py:302
  155.8 3.0 %copy.36 = f32[512,1024]{1,0:T(8,128)} copy(f32[512,1024]{0,1:T(8,128)} %bitcast.95) | data formatting | bytes 4194304 | tf_op jit(solution)/shard_map/reshape | solution.py:329
  158.8 3.2 %multiply_reduce_fusion = (f32[512]{0:T(512)S(1)}, f32[512,1024]{1,0:T(8,128)S(1)}) fusion(f32[512,1024]{1,0:T(8,128)} %copy.36, bf16[512,1024]{1,0:T(8,128)(2,1)S(1)} %copy-done.3, bf16[1024,1024]{1,0:T(8,128)(2,1)S(1)} %copy-done), kind=kOutput, calls=%fused_computation.22 | convolution fusion | flops 1078459904 | bytes 7342080 | tf_op jit(solution)/shard_map/dot_general | solution.py:273
  162.0 1.2 multiply_convert_fusion.2.refs_0_
  163.3 54.8 %shard_map.147 = bf16[512,1024]{1,0:T(8,128)(2,1)} custom-call(bf16[512,1024]{1,0:T(8,128)(2,1)} %multiply_convert_fusion.2.refs_0_, bf16[1024,1024]{1,0:T(8,128)(2,1)} %refs_1_.1), custom_call_target="tpu_custom_call" | custom-call | tf_op jit(solution)/shard_map/pallas_call | solution.py:125
  218.1 3.5 %add_convert_fusion = bf16[512,1024]{1,0:T(8,128)(2,1)} fusion(bf16[512,1024]{1,0:T(8,128)(2,1)S(1)} %copy-done.6, bf16[512,1024]{1,0:T(8,128)(2,1)} %shard_map.147, bf16[1024,1024]{1,0:T(8,128)(2,1)S(1)} %copy-done.15), kind=kOutput, calls=%fused_computation.20 | convolution fusion | flops 1075314688 | bytes 5242880 | tf_op jit(solution)/shard_map/dot_general | solution.py:343
  (53 shorter events, 0.3 us)
Async XLA Ops:
  6.5 152.2 %copy-start = (bf16[1024,1024]{1,0:T(8,128)(2,1)S(1)}, bf16[1024,1024]{1,0:T(8,128)(2,1)}, u32[]{:S(2)}) copy-start(bf16[1024,1024]{1,0:T(8,128)(2,1)} %param.20) | copy-start | bytes 6291460
  6.5 129.9 %all-gather.4.cloned.1.call-start = ((), (), s32[]{:S(2)}) async-start(), calls=%async_computation | async-start | bytes 4718592 | tf_op jit(solution)/shard_map/all_gather | solution.py:229
  6.5 55.4 %copy-start.14 = (bf16[1024,1024]{1,0:T(8,128)(2,1)S(1)}, bf16[1024,1024]{1,0:T(8,128)(2,1)}, u32[]{:S(2)}) copy-start(bf16[1024,1024]{1,0:T(8,128)(2,1)} %param.21) | copy-start | bytes 6291460
  62.0 4.6 %copy-start.2 = (bf16[512,1024]{1,0:T(8,128)(2,1)S(1)}, bf16[512,1024]{1,0:T(8,128)(2,1)}, u32[]{:S(2)}) copy-start(bf16[512,1024]{1,0:T(8,128)(2,1)} %shard_map.145) | copy-start | bytes 3145732
  62.0 4.6 %copy-start.16 = (bf16[1024,256]{1,0:T(8,128)(2,1)S(1)}, bf16[1024,256]{1,0:T(8,128)(2,1)}, u32[]{:S(2)}) copy-start(bf16[1024,256]{1,0:T(8,128)(2,1)} %param.22) | copy-start | bytes 1572868
  62.0 6.9 %copy-start.17 = (f32[16]{0:T(128)S(1)}, f32[16]{0:T(128)}, u32[]{:S(2)}) copy-start(f32[16]{0:T(128)} %param.27) | copy-start | bytes 196
  62.0 6.9 %copy-start.8 = (bf16[1024,16]{0,1:T(8,128)(2,1)S(1)}, bf16[1024,16]{0,1:T(8,128)(2,1)}, u32[]{:S(2)}) copy-start(bf16[1024,16]{0,1:T(8,128)(2,1)} %param.23) | copy-start | bytes 98308
  62.0 6.9 %copy-start.13 = (f32[16]{0:T(128)S(1)}, f32[16]{0:T(128)}, u32[]{:S(2)}) copy-start(f32[16]{0:T(128)} %param.26) | copy-start | bytes 196
  64.6 7.6 %copy-start.10 = (f32[4,1024]{1,0:T(4,128)S(1)}, f32[4,1024]{1,0:T(4,128)}, u32[]{:S(2)}) copy-start(f32[4,1024]{1,0:T(4,128)} %param.24) | copy-start | bytes 49156
  65.2 20.1 %collective-permute-start = (bf16[3,1024]{1,0:T(4,128)(2,1)}, bf16[3,1024]{1,0:T(4,128)(2,1)}, u32[]{:S(2)}, u32[]{:S(2)}) collective-permute-start(bf16[3,1024]{1,0:T(4,128)(2,1)} %slice.93), channel_id=1, source_target_pairs={{0,4},{4,8},{8,12},{12,16},{16,20},{20,24},{24,28},{1,5},{5,9},{9,... | collective-permute-start | bytes 18440 | tf_op jit(solution)/shard_map/ppermute | solution.py:224
  67.6 10.0 %collective-permute-start.1 = (bf16[3,256]{1,0:T(4,128)(2,1)}, bf16[3,256]{1,0:T(4,128)(2,1)}, u32[]{:S(2)}, u32[]{:S(2)}) collective-permute-start(bf16[3,256]{1,0:T(4,128)(2,1)} %slice.98), channel_id=1, source_target_pairs={{0,4},{4,8},{8,12},{12,16},{16,20},{20,24},{24,28},{1,5},{5,9},{9,... | collective-permute-start | bytes 4616 | tf_op jit(solution)/shard_map/ppermute | solution.py:224
  79.3 7.1 %copy-start.1 = (f32[512,1024]{1,0:T(8,128)S(1)}, f32[512,1024]{1,0:T(8,128)}, u32[]{:S(2)}) copy-start(f32[512,1024]{1,0:T(8,128)} %copy.33) | copy-start | bytes 6291460
  88.7 2.3 %copy-start.4 = (bf16[2,512,128]{2,1,0:T(8,128)(2,1)S(1)}, bf16[2,512,128]{2,1,0:T(8,128)(2,1)}, u32[]{:S(2)}) copy-start(bf16[2,512,128]{2,1,0:T(8,128)(2,1)} %shard_map.146) | copy-start | bytes 786436
  88.7 4.8 %copy-start.12 = (f32[16]{0:T(128)S(1)}, f32[16]{0:T(128)}, u32[]{:S(2)}) copy-start(f32[16]{0:T(128)} %get-tuple-element.51) | copy-start | bytes 196
  145.4 1.6 copy-start.5
  145.4 1.6 copy-start.7
  145.4 1.6 copy-start.9
  145.4 1.6 copy-start.18
  155.8 3.0 %copy-start.3 = (bf16[512,1024]{1,0:T(8,128)(2,1)S(1)}, bf16[512,1024]{1,0:T(8,128)(2,1)}, u32[]{:S(2)}) copy-start(bf16[512,1024]{1,0:T(8,128)(2,1)} %shard_map.145) | copy-start | bytes 3145732
  158.8 3.3 %copy-start.11 = (f32[1024]{0:T(1024)S(1)}, f32[1024]{0:T(1024)}, u32[]{:S(2)}) copy-start(f32[1024]{0:T(1024)} %param.29) | copy-start | bytes 12292
  163.3 54.8 %copy-start.6 = (bf16[512,1024]{1,0:T(8,128)(2,1)S(1)}, bf16[512,1024]{1,0:T(8,128)(2,1)}, u32[]{:S(2)}) copy-start(bf16[512,1024]{1,0:T(8,128)(2,1)} %refs_0_.1) | copy-start | bytes 3145732
  163.3 54.8 %copy-start.15 = (bf16[1024,1024]{1,0:T(8,128)(2,1)S(1)}, bf16[1024,1024]{1,0:T(8,128)(2,1)}, u32[]{:S(2)}) copy-start(bf16[1024,1024]{1,0:T(8,128)(2,1)} %param.31) | copy-start | bytes 6291460
Sparse Core Ops, SparseCore 0:
  93.7 42.7 all-gather.3

commit v2 on v1

--- a/solution.py
+++ b/solution.py
@@ -27,103 +27,145 @@
     pl.semaphore_wait(barrier, len(offsets))
 
 
-def send(source, target, send_sem, recv_sem, axis, peer):
-    copy = pltpu.make_async_remote_copy(
-        src_ref=source,
-        dst_ref=target,
-        send_sem=send_sem,
-        recv_sem=recv_sem,
-        device_id={axis: peer},
-        device_id_type=MESH,
-    )
-    copy.start()
-    return copy
-
-
-def project_kernel(
-    n, with_norm, width, *refs
-):
+def project_kernel(n, pieces, with_norm, width, *refs):
     if with_norm:
-        (rows_ref, gain_ref, weight_ref, out_ref, parts, arrived, own, sq_parts, sq_arrived,
-         part_send, part_recv, sq_send, sq_recv, full_send, full_recv) = refs
+        (rows_ref, gain_ref, weight_ref, out_ref, parts, inbound, back, part_send, part_recv,
+         back_recv, full_send, full_recv, squares, sq_in, sq_back, sq_send, sq_recv,
+         sq_back_recv) = refs
     else:
-        (rows_ref, weight_ref, out_ref, parts, arrived, own,
-         part_send, part_recv, full_send, full_recv) = refs
+        (rows_ref, weight_ref, out_ref, parts, inbound, back, part_send, part_recv, back_recv,
+         full_send, full_recv) = refs
     me = lax.axis_index("tp")
-    length = rows_ref.shape[0] // n
+    tokens = rows_ref.shape[0]
+    length = tokens // pieces
+    left = me < n // 2
+    inner = jnp.where(left, me + 1, me - 1)
+    outer = jnp.where(left, me - 1, me + 1)
+    end = (me == 0) | (me == n - 1)
+    middle = (me == n // 2 - 1) | (me == n // 2)
+    outer = jnp.where(end, inner, outer)
     greet("tp", range(1, n))
-    copies = []
-    own_squares = None
-    order = [o for o in sorted(range(1, n), key=lambda o: -min(o, n - o))] + [0]
-    for offset in order:
-        peer = lax.rem(me + offset, n)
-        start = pl.multiple_of(peer * length, length)
-        rows = rows_ref[pl.ds(start, length), :]
+
+    def copy(source, target, send_sem, recv_sem, peer):
+        return pltpu.make_async_remote_copy(
+            src_ref=source,
+            dst_ref=target,
+            send_sem=send_sem,
+            recv_sem=recv_sem,
+            device_id={"tp": peer},
+            device_id_type=MESH,
+        )
+
+    def sq_into():
+        return copy(squares, sq_in, sq_send, sq_recv, inner)
+
+    def sq_across():
+        return copy(squares, sq_back, sq_send, sq_back_recv, inner)
+
+    def into(k):
+        return copy(parts.at[k], inbound.at[k], part_send.at[k], part_recv.at[k], inner)
+
+    def across(k):
+        return copy(parts.at[k], back.at[k], part_send.at[k], back_recv.at[k], inner)
+
+    def outward(k):
+        rows = out_ref.at[pl.ds(k * length, length), :]
+        return copy(rows, rows, full_send.at[k], full_recv.at[k], outer)
+
+    if with_norm:
+        wide = rows_ref[...].astype(jnp.float32)
+        column = jnp.sum(wide * wide, axis=1, keepdims=True)
+        squares[...] = jnp.broadcast_to(column, (tokens, 128)).T[:8]
+
+        @pl.when(jnp.logical_not(end))
+        def _():
+            sq_into().wait_recv()
+            squares[...] += sq_in[...]
+
+        @pl.when(middle)
+        def _():
+            sq_across().start()
+
+        @pl.when(jnp.logical_not(middle))
+        def _():
+            sq_into().start()
+
+    def gather_part(k):
+        rows = rows_ref[pl.ds(k * length, length), :]
         if with_norm:
-            wide = rows.astype(jnp.float32)
-            squares = jnp.sum(wide * wide, axis=1, keepdims=True)
-            rows = (wide * gain_ref[...]).astype(jnp.bfloat16)
-            if offset:
-                spread = jnp.broadcast_to(squares, (length, 128))
-                sq_parts[offset - 1] = spread.T[:8]
-                copies.append(
-                    send(sq_parts.at[offset - 1], sq_arrived.at[offset - 1],
-                         sq_send.at[offset - 1], sq_recv.at[offset - 1], "tp", peer)
-                )
-            else:
-                own_squares = squares
+            rows = (rows.astype(jnp.float32) * gain_ref[...]).astype(jnp.bfloat16)
         part = jnp.dot(rows, weight_ref[...], preferred_element_type=jnp.float32)
-        if offset:
-            parts[offset - 1] = part.astype(jnp.bfloat16)
-            copies.append(
-                send(parts.at[offset - 1], arrived.at[offset - 1],
-                     part_send.at[offset - 1], part_recv.at[offset - 1], "tp", peer)
-            )
-        else:
-            own[...] = part
-    for copy in copies:
-        copy.wait_recv()
-    total = own[...]
-    for offset in range(1, n):
-        total = total + arrived[offset - 1].astype(jnp.float32)
+
+        @pl.when(end)
+        def _():
+            parts[k] = part.astype(jnp.bfloat16)
+
+        @pl.when(jnp.logical_not(end))
+        def _():
+            into(k).wait_recv()
+            parts[k] = (part + inbound[k].astype(jnp.float32)).astype(jnp.bfloat16)
+
+        @pl.when(middle)
+        def _():
+            across(k).start()
+
+        @pl.when(jnp.logical_not(middle))
+        def _():
+            into(k).start()
+
+    def finish_part(k):
+        @pl.when(middle)
+        def _():
+            across(k).wait_recv()
+            total = parts[k].astype(jnp.float32) + back[k].astype(jnp.float32)
+            if with_norm:
+                row = squares[:1, k * length : (k + 1) * length]
+                if k == 0:
+                    sq_across().wait_recv()
+                row = row + sq_back[:1, k * length : (k + 1) * length]
+                column = jnp.broadcast_to(row, (128, length)).T[:, :1]
+                total = total * lax.rsqrt(column / width + epsilon)
+            out_ref[pl.ds(k * length, length), :] = total.astype(jnp.bfloat16)
+
+        @pl.when(jnp.logical_not(middle))
+        def _():
+            outward(k).wait_recv()
+
+        @pl.when(jnp.logical_not(end))
+        def _():
+            outward(k).start()
+
+    lag = min(2, pieces)
+    for k in range(pieces + lag):
+        if k < pieces:
+            gather_part(k)
+        if k >= lag:
+            finish_part(k - lag)
+    for k in range(pieces):
+        into(k).wait_send()
+
+        @pl.when(jnp.logical_not(end))
+        def _():
+            outward(k).wait_send()
+
     if with_norm:
-        others = sq_arrived[0]
-        for offset in range(2, n):
-            others = others + sq_arrived[offset - 1]
-        column = jnp.broadcast_to(others[:1], (128, length)).T[:, :1]
-        factor = lax.rsqrt((own_squares + column) / width + epsilon)
-        total = total * factor
-    mine = pl.multiple_of(me * length, length)
-    out_ref[pl.ds(mine, length), :] = total.astype(jnp.bfloat16)
-    full = [
-        send(out_ref.at[pl.ds(mine, length), :], out_ref.at[pl.ds(mine, length), :],
-             full_send.at[offset - 1], full_recv.at[offset - 1], "tp", lax.rem(me + offset, n))
-        for offset in order[:-1]
-    ]
-    for copy in full:
-        copy.wait_recv()
-    for copy in copies + full:
-        copy.wait_send()
+        sq_into().wait_send()
 
 
 def project(rows, weight, gain, width, collective_id):
     n = lax.axis_size("tp")
     tokens = rows.shape[0]
-    length, rank = tokens // n, weight.shape[1]
+    pieces = 8
+    length, rank = tokens // pieces, weight.shape[1]
     vmem = pl.BlockSpec(memory_space=pltpu.VMEM)
-    sems = pltpu.SemaphoreType.DMA((n - 1,))
+    sems = pltpu.SemaphoreType.DMA((pieces,))
     with_norm = gain is not None
-    scratch = [
-        pltpu.VMEM((n - 1, length, rank), jnp.bfloat16),
-        pltpu.VMEM((n - 1, length, rank), jnp.bfloat16),
-        pltpu.VMEM((length, rank), jnp.float32),
-    ]
+    scratch = [pltpu.VMEM((pieces, length, rank), jnp.bfloat16)] * 3 + [sems] * 5
     if with_norm:
-        scratch += [pltpu.VMEM((n - 1, 8, length), jnp.float32)] * 2
-    scratch += [sems] * (6 if with_norm else 4)
+        scratch += [pltpu.VMEM((8, tokens), jnp.float32)] * 3 + [pltpu.SemaphoreType.DMA] * 3
     operands = (rows, gain[None], weight) if with_norm else (rows, weight)
     return pl.pallas_call(
-        functools.partial(project_kernel, n, with_norm, width),
+        functools.partial(project_kernel, n, pieces, with_norm, width),
         out_shape=jax.ShapeDtypeStruct((tokens, rank), jnp.bfloat16),
         in_specs=[vmem] * len(operands),
         out_specs=vmem,

time: 229 us -> 260 us (1.14)
  the two profiles are of different devices: /device:TPU:23 before, /device:TPU:6 now
where the time goes in v2:
time: 260 us; the launch traced here: 259 us
  Pallas kernels  151 us (58%)
  waiting for transfers between devices  23.4 us (9%)
  matrix products  23.1 us (9%)
  local copies, waits for them, and re-layouts  17 us (7%)
  other arithmetic  16.3 us (6%)
  between operations  13.7 us (5%)
  blocking collectives  10.8 us (4%)
  starting transfers between devices  3.82 us (1%)
    pallas_call x2, Pallas kernels, project(): pl.pallas_call(functools.partial(project_kernel, n, pieces, with_norm, wi...  143 us
    all_gather x1, waiting for transfers between devices, entering(): gathered = jax.tree.map(lambda a: lax.all_gather(a, axis), part)  23.4 us
    all_gather x1, blocking collectives, entering(): gathered = jax.tree.map(lambda a: lax.all_gather(a, axis), part)  10.8 us
    dot_general x1, matrix products, on_device(): jnp.einsum('hts,shp->thp', mixing.astype(jnp.bfloat16), narrow_values, pr...  8.8 us
    pallas_call x1, Pallas kernels, exchange(): pl.pallas_call(functools.partial(exchange_kernel, n, share), out_shape=ja...  7.71 us
    add x6, other arithmetic, combine(): later[0][:, None, None] * earlier[1] + later[1]  7.12 us
    dot_general x4, matrix products, on_device(): jnp.dot(reduced, weight, preferred_element_type=jnp.float32)  6.65 us
  transfers between devices with their start and end apart: 3, of which 1 were waited for; matrix products, arithmetic and copies ran while one was open for 6% of the time, Pallas kernels for 3%

profile of v2, /device:TPU:6, one launch (start us, length us, event | category | flops | bytes accessed | tf_op | source)
XLA Modules:
  0.0 259.3 jit_solution(3971392185401800994)
XLA Ops:
  6.5 72.9 %shard_map.145 = bf16[512,1024]{1,0:T(8,128)(2,1)} custom-call(bf16[512,1024]{1,0:T(8,128)(2,1)} %refs_0_.1, f32[1,1024]{1,0:T(1,128)} %bitcast.103, bf16[1024,1024]{1,0:T(8,128)(2,1)} %refs_2_.1), custom_call_target="tpu_custom_call" | custom-call | tf_op jit(solution)/shard_map/pallas_call | solution.py:167
  79.5 0.0 copy-start.16
  79.5 0.0 copy-start.13
  79.5 2.6 convolution_convert_fusion.1
  82.1 0.6 slice.93
  82.7 1.9 collective-permute-start
  84.7 0.4 convolution_convert_fusion.2
  85.1 0.6 slice.98
  85.7 1.9 collective-permute-start.1
  87.6 0.4 fusion.11
  88.0 0.1 compare_select_fusion.1
  88.1 1.1 reduce-window.6
  89.3 0.2 slice_reduce_fusion
  89.4 0.1 copy_bitcast_fusion
  89.5 0.7 slice_reduce_fusion.1
  90.3 0.7 bitcast_exponential_fusion
  91.0 0.8 fusion.35
  91.8 1.6 mul.217
  93.4 2.9 %copy.33 = f32[512,1024]{1,0:T(8,128)} copy(f32[512,1024]{0,1:T(8,128)} %bitcast.92) | data formatting | bytes 4194304 | tf_op jit(solution)/shard_map/mul | solution.py:351
  96.3 0.7 maximum_convert_fusion.1
  97.0 1.0 multiply_convert_fusion.7.act_ref
  98.0 7.7 %shard_map.146 = bf16[2,512,128]{2,1,0:T(8,128)(2,1)} custom-call(bf16[512,256]{1,0:T(8,128)(2,1)} %multiply_convert_fusion.7.act_ref), custom_call_target="tpu_custom_call" | custom-call | tf_op jit(solution)/shard_map/pallas_call | solution.py:247
  105.8 1.0 maximum_convert_fusion
  106.8 2.3 multiply_convert_fusion.3
  109.1 2.3 copy.34
  111.5 2.5 fusion.17
  113.9 0.0 all-gather.4.cloned.1.call-update
  114.0 10.8 %all-gather.1 = f32[8,1,16]{2,1,0:T(1,128)S(1)} all-gather(f32[1,1,16]{2,1,0:T(1,128)S(1)} %bitcast.109), channel_id=1, replica_groups=mesh['seq'=8,'tp'=4] {'seq'}, dimensions={0}, use_global_device_ids=true | all-gather | bytes 576 | tf_op jit(solution)/shard_map/all_gather | solution.py:271
  124.8 0.8 iota_compare_fusion
  125.6 1.3 fusion.20
  126.9 1.6 copy.35
  128.5 1.3 copy.30
  129.8 23.4 %all-gather.4.cloned.1.call-done = f32[128,64,128]{2,1,0:T(8,128)} async-done(((f32[16,64,128]{2,1,0:T(8,128)}), f32[128,64,128]{2,1,0:T(8,128)}) %all-gather.4.cloned.1.call-update) | async-done | bytes 4194320 | tf_op jit(solution)/shard_map/all_gather | solution.py:271
  153.3 7.6 %while.12 = (s32[]{:T(128)}, f32[16,64,128]{2,1,0:T(8,128)S(1)}, s32[]{:T(128)}, f32[8,16]{1,0:T(8,128)S(1)}, f32[8,16,64,128]{3,2,1,0:T(8,128)}, /*index=5*/s32[]{:T(128)}, s32[]{:T(128)}, s32[]{:T(128)}) while((s32[]{:T(128)}, f32[16,64,128]{2,1,0:T(8,128)S(1)}, s32[]{:T(128)}, f32[8,16]{1,0:T(8,128)S(1)}, f32[8,16,64,128]{3,2,1,0:T(8,128)}, ...), condition=%wide.region_3.4_spmd, body=%wide.region_2.3_spmd.sunk | while | flops 262149 | bytes 1573183 | solution.py:279
  153.3 1.2 bitcast_add_fusion.3
  154.6 1.2 bitcast_add_fusion.3
  155.8 1.2 bitcast_add_fusion.3
  157.0 1.2 bitcast_add_fusion.3
  158.3 1.2 bitcast_add_fusion.3
  159.5 1.2 bitcast_add_fusion.3
  160.9 0.4 fusion.15
  161.4 1.1 copy-done.5
  162.5 8.8 %fusion.9 = f32[512,16,64]{0,2,1:T(8,128)} fusion(f32[512,16,64]{0,2,1:T(8,128)S(1)} %bitcast.94, f32[512,16,64]{0,2,1:T(8,128)S(1)} %fusion.15, bf16[512,16,64]{0,2,1:T(8,128)(2,1)} %bitcast.97, f32[16,512]{1,0:T(8,128)S(1)} %get-tuple-element.68, f32[16,512]{1,0:T(8,128)S(1)} %get-tuple-element.66, f32[512,512]{1,0:T(8,128)} %fusion.20, ...), kind=kOutput, calls=%fused_computation.19 | convolution fusion | flops 564133888 | bytes 8749120 | tf_op jit(solution)/shard_map/hts,shp->thp/dot_general | solution.py:344
  171.3 3.0 %copy.36 = f32[512,1024]{1,0:T(8,128)} copy(f32[512,1024]{0,1:T(8,128)} %bitcast.95) | data formatting | bytes 4194304 | tf_op jit(solution)/shard_map/reshape | solution.py:371
  174.3 3.2 %multiply_reduce_fusion = (f32[512]{0:T(512)S(1)}, f32[512,1024]{1,0:T(8,128)S(1)}) fusion(f32[512,1024]{1,0:T(8,128)} %copy.36, bf16[512,1024]{1,0:T(8,128)(2,1)S(1)} %copy-done.3, bf16[1024,1024]{1,0:T(8,128)(2,1)S(1)} %copy-done), kind=kOutput, calls=%fused_computation.22 | convolution fusion | flops 1078459904 | bytes 7342080 | tf_op jit(solution)/shard_map/dot_general | solution.py:315
  177.6 1.2 multiply_convert_fusion.2.refs_0_
  178.8 70.2 %shard_map.147 = bf16[512,1024]{1,0:T(8,128)(2,1)} custom-call(bf16[512,1024]{1,0:T(8,128)(2,1)} %multiply_convert_fusion.2.refs_0_, bf16[1024,1024]{1,0:T(8,128)(2,1)} %refs_1_.1), custom_call_target="tpu_custom_call" | custom-call | tf_op jit(solution)/shard_map/pallas_call | solution.py:167
  249.0 3.4 %add_convert_fusion = bf16[512,1024]{1,0:T(8,128)(2,1)} fusion(bf16[512,1024]{1,0:T(8,128)(2,1)S(1)} %copy-done.6, bf16[512,1024]{1,0:T(8,128)(2,1)} %shard_map.147, bf16[1024,1024]{1,0:T(8,128)(2,1)S(1)} %copy-done.15), kind=kOutput, calls=%fused_computation.20 | convolution fusion | flops 1075314688 | bytes 5242880 | tf_op jit(solution)/shard_map/dot_general | solution.py:385
  (51 shorter events, 0.3 us)
Async XLA Ops:
  6.5 167.8 %copy-start = (bf16[1024,1024]{1,0:T(8,128)(2,1)S(1)}, bf16[1024,1024]{1,0:T(8,128)(2,1)}, u32[]{:S(2)}) copy-start(bf16[1024,1024]{1,0:T(8,128)(2,1)} %param.20) | copy-start | bytes 6291460
  6.5 146.7 %all-gather.4.cloned.1.call-start = ((), (), s32[]{:S(2)}) async-start(), calls=%async_computation | async-start | bytes 4718592 | tf_op jit(solution)/shard_map/all_gather | solution.py:271
  6.5 72.9 %copy-start.14 = (bf16[1024,1024]{1,0:T(8,128)(2,1)S(1)}, bf16[1024,1024]{1,0:T(8,128)(2,1)}, u32[]{:S(2)}) copy-start(bf16[1024,1024]{1,0:T(8,128)(2,1)} %param.21) | copy-start | bytes 6291460
  79.5 5.2 %copy-start.2 = (bf16[512,1024]{1,0:T(8,128)(2,1)S(1)}, bf16[512,1024]{1,0:T(8,128)(2,1)}, u32[]{:S(2)}) copy-start(bf16[512,1024]{1,0:T(8,128)(2,1)} %shard_map.145) | copy-start | bytes 3145732
  79.5 5.2 %copy-start.16 = (bf16[1024,256]{1,0:T(8,128)(2,1)S(1)}, bf16[1024,256]{1,0:T(8,128)(2,1)}, u32[]{:S(2)}) copy-start(bf16[1024,256]{1,0:T(8,128)(2,1)} %param.22) | copy-start | bytes 1572868
  79.5 8.1 %copy-start.17 = (f32[16]{0:T(128)S(1)}, f32[16]{0:T(128)}, u32[]{:S(2)}) copy-start(f32[16]{0:T(128)} %param.27) | copy-start | bytes 196
  79.5 8.1 %copy-start.8 = (bf16[1024,16]{0,1:T(8,128)(2,1)S(1)}, bf16[1024,16]{0,1:T(8,128)(2,1)}, u32[]{:S(2)}) copy-start(bf16[1024,16]{0,1:T(8,128)(2,1)} %param.23) | copy-start | bytes 98308
  79.5 8.1 %copy-start.13 = (f32[16]{0:T(128)S(1)}, f32[16]{0:T(128)}, u32[]{:S(2)}) copy-start(f32[16]{0:T(128)} %param.26) | copy-start | bytes 196
  82.1 8.8 %copy-start.10 = (f32[4,1024]{1,0:T(4,128)S(1)}, f32[4,1024]{1,0:T(4,128)}, u32[]{:S(2)}) copy-start(f32[4,1024]{1,0:T(4,128)} %param.24) | copy-start | bytes 49156
  82.7 23.0 %collective-permute-start = (bf16[3,1024]{1,0:T(4,128)(2,1)}, bf16[3,1024]{1,0:T(4,128)(2,1)}, u32[]{:S(2)}, u32[]{:S(2)}) collective-permute-start(bf16[3,1024]{1,0:T(4,128)(2,1)} %slice.93), channel_id=1, source_target_pairs={{0,4},{4,8},{8,12},{12,16},{16,20},{20,24},{24,28},{1,5},{5,9},{9,... | collective-permute-start | bytes 18440 | tf_op jit(solution)/shard_map/ppermute | solution.py:266
  85.7 10.6 %collective-permute-start.1 = (bf16[3,256]{1,0:T(4,128)(2,1)}, bf16[3,256]{1,0:T(4,128)(2,1)}, u32[]{:S(2)}, u32[]{:S(2)}) collective-permute-start(bf16[3,256]{1,0:T(4,128)(2,1)} %slice.98), channel_id=1, source_target_pairs={{0,4},{4,8},{8,12},{12,16},{16,20},{20,24},{24,28},{1,5},{5,9},{9,... | collective-permute-start | bytes 4616 | tf_op jit(solution)/shard_map/ppermute | solution.py:266
  98.0 8.7 %copy-start.1 = (f32[512,1024]{1,0:T(8,128)S(1)}, f32[512,1024]{1,0:T(8,128)}, u32[]{:S(2)}) copy-start(f32[512,1024]{1,0:T(8,128)} %copy.33) | copy-start | bytes 6291460
  109.1 2.3 copy-start.4
  109.1 4.8 %copy-start.12 = (f32[16]{0:T(128)S(1)}, f32[16]{0:T(128)}, u32[]{:S(2)}) copy-start(f32[16]{0:T(128)} %get-tuple-element.51) | copy-start | bytes 196
  160.9 1.6 copy-start.5
  160.9 1.6 copy-start.7
  160.9 1.6 copy-start.9
  160.9 1.6 copy-start.18
  171.3 3.0 %copy-start.3 = (bf16[512,1024]{1,0:T(8,128)(2,1)S(1)}, bf16[512,1024]{1,0:T(8,128)(2,1)}, u32[]{:S(2)}) copy-start(bf16[512,1024]{1,0:T(8,128)(2,1)} %shard_map.145) | copy-start | bytes 3145732
  174.3 3.3 %copy-start.11 = (f32[1024]{0:T(1024)S(1)}, f32[1024]{0:T(1024)}, u32[]{:S(2)}) copy-start(f32[1024]{0:T(1024)} %param.29) | copy-start | bytes 12292
  178.8 70.2 %copy-start.6 = (bf16[512,1024]{1,0:T(8,128)(2,1)S(1)}, bf16[512,1024]{1,0:T(8,128)(2,1)}, u32[]{:S(2)}) copy-start(bf16[512,1024]{1,0:T(8,128)(2,1)} %refs_0_.1) | copy-start | bytes 3145732
  178.8 70.2 %copy-start.15 = (bf16[1024,1024]{1,0:T(8,128)(2,1)S(1)}, bf16[1024,1024]{1,0:T(8,128)(2,1)}, u32[]{:S(2)}) copy-start(bf16[1024,1024]{1,0:T(8,128)(2,1)} %param.31) | copy-start | bytes 6291460
Sparse Core Ops, SparseCore 0:
  114.1 39.0 all-gather.3

commit v3 on v1

--- a/solution.py
+++ b/solution.py
@@ -224,17 +224,84 @@
     return lax.ppermute(shard, axis, pairs)
 
 
-def entering(part, axis, combine, identity):
-    place = lax.axis_index(axis)
-    gathered = jax.tree.map(lambda a: lax.all_gather(a, axis), part)
-    state = jax.tree.map(lambda a, e: jnp.zeros_like(a) + jnp.asarray(e, a.dtype), part, identity)
-
-    def one(lap, state):
-        return combine(
-            state, jax.tree.map(lambda a: lax.dynamic_index_in_dim(a, lap, 0, False), gathered)
+def states_kernel(n, own_ref, total_ref, states_ref, totals_ref, sends, recvs, tot_sends, tot_recvs):
+    place = lax.axis_index("seq")
+    greet("seq", range(1, n))
+
+    def state_copy(offset):
+        return pltpu.make_async_remote_copy(
+            src_ref=own_ref,
+            dst_ref=states_ref.at[offset - 1],
+            send_sem=sends.at[offset - 1],
+            recv_sem=recvs.at[offset - 1],
+            device_id={"seq": lax.rem(place + offset, n)},
+            device_id_type=MESH,
         )
 
-    return lax.fori_loop(0, place, one, state)
+    def total_copy(offset):
+        return pltpu.make_async_remote_copy(
+            src_ref=total_ref,
+            dst_ref=totals_ref.at[offset - 1],
+            send_sem=tot_sends.at[offset - 1],
+            recv_sem=tot_recvs.at[offset - 1],
+            device_id={"seq": lax.rem(place + offset, n)},
+            device_id_type=MESH,
+        )
+
+    for offset in range(1, n):
+
+        @pl.when(place + offset < n)
+        def _():
+            total_copy(offset).start()
+            state_copy(offset).start()
+
+    for offset in range(1, n):
+
+        @pl.when(place < offset)
+        def _():
+            states_ref[offset - 1] = jnp.zeros(own_ref.shape, own_ref.dtype)
+            totals_ref[offset - 1] = jnp.zeros(total_ref.shape, total_ref.dtype)
+
+        @pl.when(place >= offset)
+        def _():
+            total_copy(offset).wait_recv()
+            state_copy(offset).wait_recv()
+
+        @pl.when(place + offset < n)
+        def _():
+            total_copy(offset).wait_send()
+            state_copy(offset).wait_send()
+
+
+def entering(log_total, state, collective_id):
+    n = lax.axis_size("seq")
+    heads = log_total.shape[0]
+    lanes = -(-heads // 128) * 128
+    total = jnp.broadcast_to(jnp.pad(log_total, (0, lanes - heads))[None], (8, lanes))
+    own = state.reshape(-1, state.shape[-1]).astype(jnp.bfloat16)
+    vmem = pl.BlockSpec(memory_space=pltpu.VMEM)
+    sems = pltpu.SemaphoreType.DMA((n - 1,))
+    states, totals = pl.pallas_call(
+        functools.partial(states_kernel, n),
+        out_shape=(
+            jax.ShapeDtypeStruct((n - 1, *own.shape), own.dtype),
+            jax.ShapeDtypeStruct((n - 1, 8, lanes), jnp.float32),
+        ),
+        in_specs=[vmem] * 2,
+        out_specs=(vmem, vmem),
+        scratch_shapes=[sems] * 4,
+        compiler_params=pltpu.CompilerParams(
+            collective_id=collective_id, has_side_effects=True, vmem_limit_bytes=VMEM_LIMIT
+        ),
+    )(own, total)
+    logs = totals[:, 0, :heads]
+    between = jnp.exp(jnp.cumsum(jnp.pad(logs, ((1, 0), (0, 0))), axis=0)[:-1])
+    result = jnp.zeros(state.shape, jnp.float32)
+    for slot in range(n - 1):
+        result = result + between[slot][:, None, None] * states[slot].reshape(state.shape).astype(
+            jnp.float32
+        )
+    return result
 
 
 def depthwise(rim_rows, current, weights):
@@ -308,18 +375,7 @@
     ending = jnp.exp(log_decay[-1][None, :] - log_decay) * step_size
     weighted = (ending[:, :, None] * values).astype(jnp.bfloat16)
     local_state = jnp.einsum("shp,sn->hpn", weighted, inward, preferred_element_type=jnp.float32)
-    local_decay = jnp.exp(log_decay[-1])
-
-    def combine(earlier, later):
-        return (earlier[0] * later[0], later[0][:, None, None] * earlier[1] + later[1])
-
-    prefix = entering(
-        (local_decay, local_state),
-        "seq",
-        combine,
-        (jnp.ones_like(local_decay), jnp.zeros_like(local_state)),
-    )
-    incoming = prefix[1]
+    incoming = entering(log_decay[-1], local_state, 3)
     carried_in = jnp.exp(log_decay)[:, :, None] * jnp.einsum(
         "tn,hpn->thp",
         outward,

time: 229 us -> 200 us (0.87)
  Pallas kernels: 116 us -> 147 us
  waiting for transfers between devices: 24.7 us -> 0.01 us
  between operations: 13.7 us -> 0.37 us
  blocking collectives: 13.1 us -> 0 us
  local copies, waits for them, and re-layouts: 17 us -> 11.6 us
  other arithmetic: 17.5 us -> 14.4 us
    pallas_call x0 -> x1, Pallas kernels: none -> 33.1 us  [entering(): pl.pallas_call(functools.partial(states_kernel, n), out_shape=(jax.ShapeD...]
    all_gather x1 -> x0, waiting for transfers between devices: 24.6 us -> none  [entering(): gathered = jax.tree.map(lambda a: lax.all_gather(a, axis), part)]
    all_gather x1 -> x0, blocking collectives: 13.1 us -> none  [entering(): gathered = jax.tree.map(lambda a: lax.all_gather(a, axis), part)]
    add x7 -> x0, other arithmetic: 8.31 us -> none  [combine(): later[0][:, None, None] * earlier[1] + later[1]]
    convert_element_type x2 -> x0, local copies, waits for them, and re-layouts: 3.96 us -> none  [the longest x1 2.32 us: on_device(): weighted = (ending[:, :, None] * values).astype(jnp.bfloat16)]
    mul x9 -> x15, local copies, waits for them, and re-layouts: 4.55 us -> 1.01 us  [entering(): between[slot][:, None, None]]
    convert_element_type x0 -> x1, other arithmetic: none -> 3.3 us  [on_device(): incoming.astype(jnp.bfloat16)]
  transfers between devices with their start and end apart: 3 -> 2, of which waited for: 1 -> 0; matrix products, arithmetic and copies ran while one was open for 7% -> 5% of each run, Pallas kernels for 3% -> 3%
where the time goes in v3:
time: 200 us; the launch traced here: 197 us
  Pallas kernels  147 us (74%)
  matrix products  21.1 us (11%)
  other arithmetic  14.4 us (7%)
  local copies, waits for them, and re-layouts  11.6 us (6%)
  starting transfers between devices  2.56 us (1%)
    pallas_call x2, Pallas kernels, project(): pl.pallas_call(functools.partial(project_kernel, n, with_norm, width), ou...  108 us
    pallas_call x1, Pallas kernels, entering(): pl.pallas_call(functools.partial(states_kernel, n), out_shape=(jax.ShapeD...  33.1 us
    dot_general x1, matrix products, on_device(): jnp.einsum('hts,shp->thp', mixing.astype(jnp.bfloat16), narrow_values, pr...  7.2 us
    dot_general x4, matrix products, on_device(): jnp.dot(reduced, weight, preferred_element_type=jnp.float32)  6.64 us
    pallas_call x1, Pallas kernels, exchange(): pl.pallas_call(functools.partial(exchange_kernel, n, share), out_shape=ja...  5.88 us
  transfers between devices with their start and end apart: 2, of which 0 were waited for; matrix products, arithmetic and copies ran while one was open for 5% of the time, Pallas kernels for 3%

profile of v3, /device:TPU:23, one launch (start us, length us, event | category | flops | bytes accessed | tf_op | source)
XLA Modules:
  0.0 197.4 jit_solution(495302790692744364)
XLA Ops:
  0.0 55.4 %shard_map.145 = bf16[512,1024]{1,0:T(8,128)(2,1)} custom-call(bf16[512,1024]{1,0:T(8,128)(2,1)} %refs_0_.1, f32[1,1024]{1,0:T(1,128)} %bitcast.110, bf16[1024,1024]{1,0:T(8,128)(2,1)} %refs_2_.1), custom_call_target="tpu_custom_call" | custom-call | tf_op jit(solution)/shard_map/pallas_call | solution.py:125
  55.5 2.6 %convolution_convert_fusion.1 = bf16[512,1024]{1,0:T(8,128)(2,1)S(1)} fusion(bf16[512,1024]{1,0:T(8,128)(2,1)} %shard_map.145, bf16[1024,1024]{1,0:T(8,128)(2,1)S(1)} %copy-done.16), kind=kOutput, calls=%fused_computation.26 | convolution fusion | flops 1074266112 | bytes 4194304 | tf_op jit(solution)/shard_map/dot_general | solution.py:340
  58.1 1.0 copy-done.4
  59.0 0.6 slice.157
  59.6 1.3 collective-permute-start
  60.9 0.4 convolution_convert_fusion.3
  61.4 0.6 slice.162
  62.0 1.3 collective-permute-start.1
  63.3 0.4 fusion.12
  63.7 0.1 compare_select_fusion.1
  63.8 1.1 reduce-window.9
  64.9 0.2 slice_reduce_fusion
  65.1 0.7 copy_bitcast_fusion
  65.8 0.2 slice_reduce_fusion.1
  66.0 0.7 bitcast_exponential_fusion
  66.7 0.8 fusion.34
  67.5 0.8 iota_compare_fusion
  68.3 0.6 pad.6
  68.9 0.7 maximum_convert_fusion.1
  69.6 1.0 multiply_convert_fusion.6.act_ref
  70.6 5.9 %shard_map.146 = bf16[2,512,128]{2,1,0:T(8,128)(2,1)} custom-call(bf16[512,256]{1,0:T(8,128)(2,1)} %multiply_convert_fusion.6.act_ref), custom_call_target="tpu_custom_call" | custom-call | tf_op jit(solution)/shard_map/pallas_call | solution.py:205
  76.5 2.3 %fusion.19 = f32[512,512]{1,0:T(8,128)} fusion(bf16[2,512,128]{2,1,0:T(8,128)(2,1)} %shard_map.146), kind=kOutput, calls=%fused_computation.47 | convolution fusion | flops 67108864 | bytes 1310720 | tf_op jit(solution)/shard_map/dot_general | solution.py:360
  78.8 1.0 maximum_convert_fusion
  79.8 2.2 %multiply_convert_fusion.3 = bf16[512,1024]{1,0:T(8,128)(2,1)} fusion(f32[515,1024]{1,0:T(8,128)S(1)} %maximum_convert_fusion, f32[1024]{0:T(1024)S(1)} %bitcast.107, f32[1024]{0:T(1024)S(1)} %bitcast.108, f32[1024]{0:T(1024)S(1)} %bitcast.106, f32[1024]{0:T(1024)S(1)} %bitcast.105), kind=kLoop, calls=%fused_computation.24 | loop fusion | flops 6291456 | bytes 9453568 | tf_op jit(solution)/shard_map/convert_element_type | solution.py:313
  82.0 2.3 %copy.21 = bf16[512,1024]{0,1:T(8,128)(2,1)} copy(bf16[512,1024]{1,0:T(8,128)(2,1)} %multiply_convert_fusion.3) | data formatting | bytes 2097152 | tf_op jit(solution)/shard_map/convert_element_type | solution.py:313
  84.4 1.4 fusion.2
  85.8 1.1 convolution_convert_fusion.2.own_ref
  87.0 0.6 broadcast_in_dim.25.total_ref
  87.5 33.1 %shard_map.147 = (bf16[7,1024,128]{2,1,0:T(8,128)(2,1)}, f32[7,8,128]{2,1,0:T(8,128)}) custom-call(bf16[1024,128]{1,0:T(8,128)(2,1)} %convolution_convert_fusion.2.own_ref, f32[8,128]{1,0:T(8,128)} %broadcast_in_dim.25.total_ref), custom_call_target="tpu_custom_call" | custom-call | tf_op jit(solution)/shard_map/pallas_call | solution.py:284
  120.6 0.8 slice.141
  121.4 0.1 mul.337
  121.5 0.1 mul.338
  121.6 0.1 mul.332
  121.6 0.1 mul.333
  121.7 0.1 mul.327
  121.8 0.1 mul.328
  121.9 0.1 mul.323
  122.1 0.1 mul.318
  122.2 0.1 mul.313
  122.3 0.1 mul.308
  122.5 3.3 %add_convert_fusion.1 = bf16[1,1024,128]{2,1,0:T(8,128)(2,1)S(1)} fusion(bf16[7,1024,128]{2,1,0:T(8,128)(2,1)} %get-tuple-element.8, f32[1024]{0:T(1024)S(1)} %mul.338, f32[1024]{0:T(1024)S(1)} %mul.333, f32[1024]{0:T(1024)S(1)} %mul.328, f32[1024]{0:T(1024)S(1)} %mul.323, f32[1024]{0:T(1024)S(1)} %mul.318, f32[1024]{0:T(1024)S(1)} %mul.313, f32[1024]{0:T(1024)S(1)} %mul.308), kind=kLoop, calls=%fused_computation.41 | loop fusion | flops 2752512 | bytes 2125824 | tf_op jit(solution)/shard_map/convert_element_type | solution.py:382
  125.8 0.4 fusion.16
  126.3 7.2 %fusion.3 = f32[512,16,64]{0,2,1:T(8,128)} fusion(bf16[512,16,64]{0,2,1:T(8,128)(2,1)S(1)} %bitcast.100, f32[512,16,64]{0,2,1:T(8,128)S(1)} %fusion.16, f32[16,512]{1,0:T(8,128)S(1)} %get-tuple-element.13, f32[16,512]{1,0:T(8,128)S(1)} %copy-done.10, f32[512,512]{1,0:T(8,128)S(1)} %copy-done.7, pred[512,512]{1,0:T(8,128)(4,1)S(1)} %copy-done.8, ...), kind=kOutput, calls=%fused_computation.8 | convolution fusion | flops 564658176 | bytes 6651968 | tf_op jit(solution)/shard_map/hts,shp->thp/dot_general | solution.py:369
  133.5 2.9 %copy.24 = f32[512,1024]{1,0:T(8,128)} copy(f32[512,1024]{0,1:T(8,128)} %bitcast.102) | data formatting | bytes 4194304 | tf_op jit(solution)/shard_map/reshape | solution.py:385
  136.4 3.3 %multiply_reduce_fusion = (f32[512]{0:T(512)S(1)}, f32[512,1024]{1,0:T(8,128)S(1)}) fusion(f32[512,1024]{1,0:T(8,128)} %copy.24, bf16[512,1024]{1,0:T(8,128)(2,1)S(1)} %copy-done.1, bf16[1024,1024]{1,0:T(8,128)(2,1)S(1)} %copy-done), kind=kOutput, calls=%fused_computation.23 | convolution fusion | flops 1078459904 | bytes 7342080 | tf_op jit(solution)/shard_map/dot_general | solution.py:340
  139.6 1.2 multiply_convert_fusion.2.refs_0_
  140.9 53.0 %shard_map.148 = bf16[512,1024]{1,0:T(8,128)(2,1)} custom-call(bf16[512,1024]{1,0:T(8,128)(2,1)} %multiply_convert_fusion.2.refs_0_, bf16[1024,1024]{1,0:T(8,128)(2,1)} %refs_1_.1), custom_call_target="tpu_custom_call" | custom-call | tf_op jit(solution)/shard_map/pallas_call | solution.py:125
  193.9 3.5 %add_convert_fusion = bf16[512,1024]{1,0:T(8,128)(2,1)} fusion(bf16[512,1024]{1,0:T(8,128)(2,1)S(1)} %copy-done.6, bf16[512,1024]{1,0:T(8,128)(2,1)} %shard_map.148, bf16[1024,1024]{1,0:T(8,128)(2,1)S(1)} %copy-done.17), kind=kOutput, calls=%fused_computation.21 | convolution fusion | flops 1075314688 | bytes 5242880 | tf_op jit(solution)/shard_map/dot_general | solution.py:399
  (57 shorter events, 0.5 us)
Async XLA Ops:
  0.0 136.4 %copy-start = (bf16[1024,1024]{1,0:T(8,128)(2,1)S(1)}, bf16[1024,1024]{1,0:T(8,128)(2,1)}, u32[]{:S(2)}) copy-start(bf16[1024,1024]{1,0:T(8,128)(2,1)} %param.18) | copy-start | bytes 6291460
  0.0 55.4 %copy-start.16 = (bf16[1024,1024]{1,0:T(8,128)(2,1)S(1)}, bf16[1024,1024]{1,0:T(8,128)(2,1)}, u32[]{:S(2)}) copy-start(bf16[1024,1024]{1,0:T(8,128)(2,1)} %param.19) | copy-start | bytes 6291460
  55.4 5.5 %copy-start.1 = (bf16[512,1024]{1,0:T(8,128)(2,1)S(1)}, bf16[512,1024]{1,0:T(8,128)(2,1)}, u32[]{:S(2)}) copy-start(bf16[512,1024]{1,0:T(8,128)(2,1)} %shard_map.145) | copy-start | bytes 3145732
  55.4 5.5 %copy-start.18 = (bf16[1024,256]{1,0:T(8,128)(2,1)S(1)}, bf16[1024,256]{1,0:T(8,128)(2,1)}, u32[]{:S(2)}) copy-start(bf16[1024,256]{1,0:T(8,128)(2,1)} %param.20) | copy-start | bytes 1572868
  55.4 7.8 %copy-start.12 = (f32[4,1024]{1,0:T(4,128)S(1)}, f32[4,1024]{1,0:T(4,128)}, u32[]{:S(2)}) copy-start(f32[4,1024]{1,0:T(4,128)} %param.22) | copy-start | bytes 49156
  55.4 7.8 %copy-start.19 = (f32[16]{0:T(128)S(1)}, f32[16]{0:T(128)}, u32[]{:S(2)}) copy-start(f32[16]{0:T(128)} %param.25) | copy-start | bytes 196
  55.5 7.8 %copy-start.9 = (bf16[1024,16]{0,1:T(8,128)(2,1)S(1)}, bf16[1024,16]{0,1:T(8,128)(2,1)}, u32[]{:S(2)}) copy-start(bf16[1024,16]{0,1:T(8,128)(2,1)} %param.21) | copy-start | bytes 98308
  55.5 7.8 %copy-start.14 = (f32[16]{0:T(128)S(1)}, f32[16]{0:T(128)}, u32[]{:S(2)}) copy-start(f32[16]{0:T(128)} %param.24) | copy-start | bytes 196
  58.1 1.0 copy-start.4
  59.6 19.1 %collective-permute-start = (bf16[3,1024]{1,0:T(4,128)(2,1)}, bf16[3,1024]{1,0:T(4,128)(2,1)}, u32[]{:S(2)}, u32[]{:S(2)}) collective-permute-start(bf16[3,1024]{1,0:T(4,128)(2,1)} %slice.157), channel_id=1, source_target_pairs={{0,4},{4,8},{8,12},{12,16},{16,20},{20,24},{24,28},{1,5},{5,9},{9,... | collective-permute-start | bytes 18440 | tf_op jit(solution)/shard_map/ppermute | solution.py:224
  62.0 6.9 %collective-permute-start.1 = (bf16[3,256]{1,0:T(4,128)(2,1)}, bf16[3,256]{1,0:T(4,128)(2,1)}, u32[]{:S(2)}, u32[]{:S(2)}) collective-permute-start(bf16[3,256]{1,0:T(4,128)(2,1)} %slice.162), channel_id=1, source_target_pairs={{0,4},{4,8},{8,12},{12,16},{16,20},{20,24},{24,28},{1,5},{5,9},{9,... | collective-permute-start | bytes 4616 | tf_op jit(solution)/shard_map/ppermute | solution.py:224
  69.6 9.2 %copy-start.5 = (bf16[512,1024]{1,0:T(8,128)(2,1)S(1)}, bf16[512,1024]{1,0:T(8,128)(2,1)}, u32[]{:S(2)}) copy-start(bf16[512,1024]{1,0:T(8,128)(2,1)} %copy-done.4) | copy-start | bytes 3145732
  82.0 3.8 %copy-start.3 = (bf16[2,512,128]{2,1,0:T(8,128)(2,1)S(1)}, bf16[2,512,128]{2,1,0:T(8,128)(2,1)}, u32[]{:S(2)}) copy-start(bf16[2,512,128]{2,1,0:T(8,128)(2,1)} %shard_map.146) | copy-start | bytes 786436
  84.4 2.6 %copy-start.15 = (f32[128]{0:T(128)S(1)}, f32[128]{0:T(128)}, u32[]{:S(2)}) copy-start(f32[128]{0:T(128)} %pad.6) | copy-start | bytes 1540
  122.4 3.8 %copy-start.2 = (bf16[512,1024]{0,1:T(8,128)(2,1)S(1)}, bf16[512,1024]{0,1:T(8,128)(2,1)}, u32[]{:S(2)}) copy-start(bf16[512,1024]{0,1:T(8,128)(2,1)} %copy.21) | copy-start | bytes 3145732
  122.4 3.8 %copy-start.7 = (f32[512,512]{1,0:T(8,128)S(1)}, f32[512,512]{1,0:T(8,128)}, u32[]{:S(2)}) copy-start(f32[512,512]{1,0:T(8,128)} %fusion.19) | copy-start | bytes 3145732
  122.4 3.8 %copy-start.8 = (pred[512,512]{1,0:T(8,128)(4,1)S(1)}, pred[512,512]{1,0:T(8,128)(4,1)}, u32[]{:S(2)}) copy-start(pred[512,512]{1,0:T(8,128)(4,1)} %iota_compare_fusion) | copy-start | bytes 786436
  122.4 3.8 %copy-start.10 = (f32[16,512]{1,0:T(8,128)S(1)}, f32[16,512]{1,0:T(8,128)}, u32[]{:S(2)}) copy-start(f32[16,512]{1,0:T(8,128)} %get-tuple-element.11) | copy-start | bytes 98308
  122.4 3.8 %copy-start.11 = (f32[512,16]{0,1:T(8,128)S(1)}, f32[512,16]{0,1:T(8,128)}, u32[]{:S(2)}) copy-start(f32[512,16]{0,1:T(8,128)} %get-tuple-element.9) | copy-start | bytes 98308
  122.5 3.8 %copy-start.20 = (f32[16]{0:T(128)S(1)}, f32[16]{0:T(128)}, u32[]{:S(2)}) copy-start(f32[16]{0:T(128)} %param.26) | copy-start | bytes 196
  136.4 3.3 %copy-start.13 = (f32[1024]{0:T(1024)S(1)}, f32[1024]{0:T(1024)}, u32[]{:S(2)}) copy-start(f32[1024]{0:T(1024)} %param.27) | copy-start | bytes 12292
  140.9 53.1 %copy-start.6 = (bf16[512,1024]{1,0:T(8,128)(2,1)S(1)}, bf16[512,1024]{1,0:T(8,128)(2,1)}, u32[]{:S(2)}) copy-start(bf16[512,1024]{1,0:T(8,128)(2,1)} %refs_0_.1) | copy-start | bytes 3145732
  140.9 53.1 %copy-start.17 = (bf16[1024,1024]{1,0:T(8,128)(2,1)S(1)}, bf16[1024,1024]{1,0:T(8,128)(2,1)}, u32[]{:S(2)}) copy-start(bf16[1024,1024]{1,0:T(8,128)(2,1)} %param.29) | copy-start | bytes 6291460
